TPU v7x, 32 devices: a whole 2x2x4 slice. The times are simulated.
32 devices in a mesh: clu: 16 (over z, x, core), doc: 2 (over y).
Axes of the slice: x: 2, y: 2, z: 4, core: 2. Of those that a mesh axis runs over, the one named last changes fastest.
Arguments:
- docs: bfloat16 [8192, 768], P(('clu', 'doc')), may hold values from -6 to 6
- centroids: bfloat16 [5504, 768], P('doc', 'clu'), may hold values from -6 to 6
- assigned: int32 [8192], P(('clu', 'doc')), may hold values from 0 to 5503
Outputs:
- nearest: float32 [8192], P(('clu', 'doc'))
- assigned_dist: float32 [8192], P(('clu', 'doc'))
Inputs may be any that keep to these rules, and one draw needn't show every extreme that they name: `assigned`: cluster ids.
All inputs are finite; a program needn't handle non-finite values.
Results may differ from a plain program's by a relative error of at most 0.0003.
Values may be sent and summed in bfloat16 or wider, within the bound.
A program may use at most 64 MiB of HBM per device.

v0:
```python
import functools

import jax
import jax.numpy as jnp
from jax import lax
from jax.experimental import pallas as pl
from jax.experimental.pallas import tpu as pltpu
from jax.sharding import PartitionSpec as P

epsilon = 1e-06
PIECES = 4
ROWS = 64
MESH = pl.DeviceIdType.MESH


def chip_at(pos, n):
    half = n // 2
    return jnp.where(pos < half, 2 * pos, 2 * (n - 1 - pos) + 1)


def cut(width):
    tiles = (width + 127) // 128
    ends = [min(-(-tiles * (c + 1) // PIECES) * 128, width) for c in range(PIECES)]
    return tuple((a, b - a) for a, b in zip([0] + ends[:-1], ends))


def kernel(n, nd, feat, docs_in, cents_in, ids_in, near_out, chosen_out,
           buf, docs_all, ids_all, dp_a, dp_b, dp_c, acc, idb, mx, ch, csq, scale, res, got,
           local_sem, ring_send, pair_send, recv, docs_send, docs_recv, ids_send, ids_recv,
           res_send, res_recv):
    hops = n // 2
    fp = cents_in.shape[0]
    width = cents_in.shape[1]
    rows_dev = docs_in.shape[0]
    chunks = cut(width)
    half = len(chunks) // 2

    clu, doc = lax.axis_index("clu"), lax.axis_index("doc")
    core, chip = lax.rem(clu, 2), lax.div(clu, 2)
    z, x = lax.div(chip, 2), lax.rem(chip, 2)
    pos = jnp.where(x == 0, z, n - 1 - z)
    right = chip_at(lax.rem(pos + 1, n), n) * 2 + core
    left = chip_at(lax.rem(pos + n - 1, n), n) * 2 + core
    partner = chip * 2 + (1 - core)

    own_c = pltpu.make_async_copy(cents_in, buf.at[pl.ds(0, fp), :], local_sem.at[0])
    own_d = pltpu.make_async_copy(docs_in, docs_all.at[0], local_sem.at[1])
    own_i = pltpu.make_async_copy(ids_in, ids_all.at[0], local_sem.at[2])
    own_c.start()
    own_d.start()
    own_i.start()

    barrier = pltpu.get_barrier_semaphore()
    for peer in (left, right, partner):
        pl.semaphore_signal(barrier, inc=1, device_id={"clu": peer}, device_id_type=MESH)
    for k in range(1, nd):
        pl.semaphore_signal(barrier, inc=1, device_id={"doc": lax.rem(doc + k, nd)}, device_id_type=MESH)
    pl.semaphore_wait(barrier, 3 + nd - 1)

    def slot(way, h):
        if h == 0:
            return 0
        if h == hops:
            return n - 1
        return 2 * h - 1 if way == 0 else 2 * h

    def piece(s, m, c):
        return buf.at[pl.ds((2 * s + m) * fp, fp), pl.ds(*chunks[c])]

    def reach(way, c):
        return hops if way == c // half else hops - 1

    sent = []

    def ring(way, h, c):
        s, t = slot(way, h), slot(way, h + 1)
        copy = pltpu.make_async_remote_copy(
            src_ref=piece(s, 0, c), dst_ref=piece(t, 0, c),
            send_sem=ring_send.at[way, h, c], recv_sem=recv.at[t, 0, c],
            device_id={"clu": right if way == 0 else left}, device_id_type=MESH)
        copy.start()
        sent.append(copy)

    def share(s, c):
        copy = pltpu.make_async_remote_copy(
            src_ref=piece(s, 0, c), dst_ref=piece(s, 1, c),
            send_sem=pair_send.at[s, c], recv_sem=recv.at[s, 1, c],
            device_id={"clu": partner}, device_id_type=MESH)
        copy.start()
        sent.append(copy)

    def landed(s, m, c):
        pltpu.make_async_remote_copy(
            src_ref=piece(s, m, c), dst_ref=piece(s, m, c),
            send_sem=pair_send.at[s, c], recv_sem=recv.at[s, m, c],
            device_id={"clu": partner}, device_id_type=MESH).wait_recv()

    own_c.wait()
    for i in range(PIECES):
        ring(0, 0, i)
        ring(1, 0, (i + half) % PIECES)
    for c in range(PIECES):
        share(0, c)
    own_d.wait()
    own_i.wait()
    doc_copies = []
    for k in range(1, nd):
        mate = lax.rem(doc + k, nd)
        for ref, ss, rs in ((ids_all, ids_send, ids_recv), (docs_all, docs_send, docs_recv)):
            copy = pltpu.make_async_remote_copy(
                src_ref=ref.at[0], dst_ref=ref.at[k], send_sem=ss.at[k], recv_sem=rs.at[k],
                device_id={"doc": mate}, device_id_type=MESH)
            copy.start()
            doc_copies.append(copy)

    def owner(s):
        if s == 0:
            p = pos
        elif s == n - 1:
            p = pos + hops
        elif s % 2:
            p = pos + n - (s + 1) // 2
        else:
            p = pos + s // 2
        return chip_at(lax.rem(p, n), n)

    ranges = ((0, n - 3), (n - 3, n - 1), (n - 1, n))
    spread = (dp_a, dp_b, dp_c)

    def permute(k):
        rows = docs_all[k]
        for (first, last), out in zip(ranges, spread):
            wide = out.shape[1]
            lane = lax.broadcasted_iota(jnp.int32, (1, wide), 1)
            target = jnp.full((1, wide), -1, jnp.int32)
            for s in range(first, last):
                chip_s = owner(s)
                for m in (0, 1):
                    part = chip_s * 2 + (core if m == 0 else 1 - core)
                    start = (2 * (s - first) + m) * fp
                    inside = (lane >= start) & (lane < start + feat)
                    target = jnp.where(inside, lane - start + part * feat, target)
            source = lax.broadcasted_iota(jnp.int32, (rows.shape[1], wide), 0)
            mover = jnp.where(source == target, 1.0, 0.0).astype(jnp.bfloat16)
            out[pl.ds(k * rows_dev, rows_dev), :] = jnp.dot(
                rows, mover, preferred_element_type=jnp.float32).astype(jnp.bfloat16)

    def prepare_ids(k):
        base = doc * width
        ids = ids_all[k] - base
        ids = jnp.where((ids >= 0) & (ids < width), ids, -1)
        full = jnp.broadcast_to(ids, (128, rows_dev)).T
        lanes = lax.broadcasted_iota(jnp.int32, (rows_dev, 128), 1)
        idb[pl.ds(k * rows_dev, rows_dev), :] = jnp.where(full >= 0, full - lanes, -(2**20))

    def phase(index, c):
        first, last = ranges[index]
        start, depth = 2 * first * fp, 2 * (last - first) * fp
        cols = pl.ds(*chunks[c])
        block = buf[pl.ds(start, depth), cols]
        prod = jnp.dot(spread[index][...], block, preferred_element_type=jnp.float32)
        w32 = block.astype(jnp.float32)
        sq = jnp.sum((w32 * w32).reshape(depth // 8, 8, chunks[c][1]), 0)
        if index == 0:
            acc[:, cols] = prod
            csq[:, cols] = sq
        else:
            acc[:, cols] += prod
            csq[:, cols] += sq

    tail = pl.ds(2 * (n - 1) * fp, 2 * fp)

    def finish_scale(c):
        cols = pl.ds(*chunks[c])
        w32 = buf[tail, cols].astype(jnp.float32)
        sq = jnp.sum((w32 * w32).reshape(2 * fp // 8, 8, chunks[c][1]), 0) + csq[:, cols]
        scale[:, cols] = lax.rsqrt(jnp.sum(sq, 0, keepdims=True) + epsilon)

    def final(k, c):
        start, wide = chunks[c]
        prod = jnp.dot(dp_c[pl.ds(k * rows_dev, rows_dev), :], buf[tail, pl.ds(start, wide)],
                       preferred_element_type=jnp.float32)
        for r in range(0, rows_dev, ROWS):
            rs = pl.ds(k * rows_dev + r, ROWS)
            top, hit = mx[rs, :], ch[rs, :]
            ids = idb[rs, :]
            for a in range(0, wide, 128):
                w = min(128, wide - a)
                cols = pl.ds(start + a, w)
                v = (acc[rs, cols] + prod[r:r + ROWS, a:a + w]) * scale[:, cols]
                if w == 128:
                    top = jnp.maximum(top, v)
                    hit = jnp.where(ids == start + a, v, hit)
                else:
                    mx[rs, :] = top
                    ch[rs, :] = hit
                    mx[rs, pl.ds(0, w)] = jnp.maximum(mx[rs, pl.ds(0, w)], v)
                    ch[rs, pl.ds(0, w)] = jnp.where(idb[rs, pl.ds(0, w)] == start + a, v, ch[rs, pl.ds(0, w)])
            if wide % 128 == 0:
                mx[rs, :] = top
                ch[rs, :] = hit

    def reduced(k):
        rs = pl.ds(k * rows_dev, rows_dev)
        return (jnp.max(mx[rs, :].T, 0, keepdims=True), jnp.sum(ch[rs, :].T, 0, keepdims=True))

    mx[...] = jnp.full(mx.shape, -3.0e38, jnp.float32)
    ch[...] = jnp.zeros(ch.shape, jnp.float32)
    permute(0)
    prepare_ids(0)
    wide = docs_all[0].astype(jnp.float32)
    squares = wide * wide
    total = squares[:, 0:128]
    for a in range(128, wide.shape[1], 128):
        total = total + squares[:, a:a + 128]
    scale_x = lax.rsqrt(jnp.sum(total.T, 0, keepdims=True) + epsilon)

    def step(way, h, c):
        s = slot(way, h)
        landed(s, 0, c)
        if h < reach(way, c):
            ring(way, h, c)
        share(s, c)

    def pair(h, i):
        step(0, h, i)
        step(1, h, (i + half) % PIECES)

    def partners(slots, c):
        for s in slots:
            landed(s, 1, c)

    early, late = range(n - 3), (n - 3, n - 2)
    order = [j // 2 + half * (j % 2) for j in range(PIECES)]
    for h in range(1, hops):
        for i in range(PIECES):
            pair(h, i)
            if h == hops - 2 and i == half:
                for copy in doc_copies:
                    copy.wait()
                for k in range(1, nd):
                    permute(k)
                    prepare_ids(k)
            if h == hops - 1:
                c = order[i]
                partners(early, c)
                phase(0, c)
    for c in order[:half]:
        partners(late, c)
        phase(1, c)
    for i in range(half):
        for way in (0, 1):
            c = i + half * way
            landed(n - 1, 0, c)
            share(n - 1, c)
    for c in order[half:]:
        partners(late, c)
        phase(1, c)
    for c in order[:-2]:
        landed(n - 1, 1, c)
        finish_scale(c)
        for k in range(nd):
            final(k, c)
    for c in order[-2:]:
        landed(n - 1, 1, c)
        finish_scale(c)

    returns = []
    for k in range(1, nd):
        for c in order[-2:]:
            final(k, c)
        best, chosen = reduced(k)
        res[k, 0:1, :] = best
        res[k, 1:2, :] = chosen
        copy = pltpu.make_async_remote_copy(
            src_ref=res.at[k], dst_ref=got.at[k], send_sem=res_send.at[k], recv_sem=res_recv.at[k],
            device_id={"doc": lax.rem(doc + nd - k, nd)}, device_id_type=MESH)
        copy.start()
        returns.append(copy)
    for c in order[-2:]:
        final(0, c)
    best, chosen = reduced(0)
    for k in range(1, nd):
        returns[k - 1].wait()
        best = jnp.maximum(best, got[k, 0:1, :])
        chosen = chosen + got[k, 1:2, :]
    near_out[...] = best * scale_x
    chosen_out[...] = chosen * scale_x
    for copy in sent:
        copy.wait_send()


def on_device(docs, centroids, assigned):
    n_clu, nd = lax.axis_size("clu"), lax.axis_size("doc")
    n = n_clu // 2
    rows_dev, depth = docs.shape
    width, feat = centroids.shape
    fp = (feat + 15) // 16 * 16
    cents = centroids.T
    if fp != feat:
        cents = jnp.pad(cents, ((0, fp - feat), (0, 0)))
    rows = nd * rows_dev
    any_space = pl.BlockSpec(memory_space=pl.ANY)
    vmem = pl.BlockSpec(memory_space=pltpu.VMEM)
    dma = pltpu.SemaphoreType.DMA
    hops = n // 2
    line = jax.ShapeDtypeStruct((1, rows_dev), jnp.float32)
    near, chosen = pl.pallas_call(
        functools.partial(kernel, n, nd, feat),
        out_shape=(line, line),
        in_specs=[any_space] * 3,
        out_specs=(vmem, vmem),
        scratch_shapes=[
            pltpu.VMEM((n_clu * fp, width), jnp.bfloat16),
            pltpu.VMEM((nd, rows_dev, depth), jnp.bfloat16),
            pltpu.VMEM((nd, 1, rows_dev), jnp.int32),
            pltpu.VMEM((rows, (n - 3) * 2 * fp), jnp.bfloat16),
            pltpu.VMEM((rows, 4 * fp), jnp.bfloat16),
            pltpu.VMEM((rows, 2 * fp), jnp.bfloat16),
            pltpu.VMEM((rows, width), jnp.float32),
            pltpu.VMEM((rows, 128), jnp.int32),
            pltpu.VMEM((rows, 128), jnp.float32),
            pltpu.VMEM((rows, 128), jnp.float32),
            pltpu.VMEM((8, width), jnp.float32),
            pltpu.VMEM((1, width), jnp.float32),
            pltpu.VMEM((nd, 2, rows_dev), jnp.float32),
            pltpu.VMEM((nd, 2, rows_dev), jnp.float32),
            dma((3,)),
            dma((2, hops, PIECES)),
            dma((n, PIECES)),
            dma((n, 2, PIECES)),
            dma((nd,)), dma((nd,)), dma((nd,)), dma((nd,)), dma((nd,)), dma((nd,)),
        ],
        compiler_params=pltpu.CompilerParams(collective_id=0, has_side_effects=True),
        name="ring_distances",
    )(docs, cents, assigned.reshape(1, rows_dev))
    return 1.0 - near.reshape(rows_dev), 1.0 - chosen.reshape(rows_dev)


def solution(mesh):
    placed = (P(("clu", "doc"), None), P("doc", "clu"), P(("clu", "doc")))
    return jax.shard_map(
        on_device,
        mesh=mesh,
        in_specs=placed,
        out_specs=(P(("clu", "doc")), P(("clu", "doc"))),
        check_vma=False,
    )
```

profile of v0, /device:TPU:0, one launch (start us, length us, event | category | flops | bytes accessed | tf_op | source)
XLA Modules:
  0.0 34.5 jit_solution(5199725418724960359)
XLA Ops:
  0.6 32.6 %ring_distances.1 = (f32[1,256]{1,0:T(1,128)}, f32[1,256]{1,0:T(1,128)}) custom-call(bf16[256,768]{1,0:T(8,128)(2,1)} %docs_in.1, bf16[48,2752]{1,0:T(8,128)(2,1)} %bitcast.4, s32[1,256]{1,0:T(1,128)} %bitcast.5), custom_call_target="tpu_custom_call" | custom-call | tf_op jit(solution)/shard_map/ring_distances/pallas_call | solution.py:308
  33.2 0.0 copy-start.1
  33.3 0.0 copy-start
  33.3 0.6 %copy-done.1 = f32[1,256]{1,0:T(1,128)S(1)} copy-done((f32[1,256]{1,0:T(1,128)S(1)}, f32[1,256]{1,0:T(1,128)}, u32[]{:S(2)}) %copy-start.1) | copy-done | bytes 1048
  33.9 0.0 copy-done
  33.9 0.6 %broadcast_subtract_fusion = (f32[1,256]{1,0:T(1,128)}, f32[1,256]{1,0:T(1,128)}) fusion(f32[1,256]{1,0:T(1,128)S(1)} %copy-done.1, f32[1,256]{1,0:T(1,128)S(1)} %copy-done), kind=kLoop, calls=%fused_computation | loop fusion | flops 512 | bytes 4096 | tf_op jit(solution)/shard_map/sub | solution.py:337
Async XLA Ops:
  33.2 0.6 %copy-start.1 = (f32[1,256]{1,0:T(1,128)S(1)}, f32[1,256]{1,0:T(1,128)}, u32[]{:S(2)}) copy-start(f32[1,256]{1,0:T(1,128)} %get-tuple-element.5) | copy-start | bytes 3076
  33.3 0.6 %copy-start = (f32[1,256]{1,0:T(1,128)S(1)}, f32[1,256]{1,0:T(1,128)}, u32[]{:S(2)}) copy-start(f32[1,256]{1,0:T(1,128)} %get-tuple-element.4) | copy-start | bytes 3076
where the time goes:
time: 34.6 us; the launch traced here: 34.5 us
  Pallas kernels  32.6 us (94%)
  between operations  0.65 us (2%)
  local copies, waits for them, and re-layouts  0.63 us (2%)
  other arithmetic  0.57 us (2%)
    pallas_call x1, Pallas kernels, on_device(): pl.pallas_call(functools.partial(kernel, n, nd, feat), out_shape=(line, l...  32.6 us

commit v1 on v0

--- a/solution.py
+++ b/solution.py
@@ -290,7 +290,368 @@
         copy.wait_send()
 
 
+def layer_kernel(nz, feat, docs_in, cents_in, ids_in, near_out, chosen_out,
+                 own, raw, buf, docs, ids, acc, idb, csq, scale, res, got,
+                 local_sem, c_send, c_recv, z_send, d_send, d_recv, i_send, i_recv, r_send, r_recv):
+    width = cents_in.shape[1]
+    rows_dev, depth = docs_in.shape
+    tiles = own.shape[1] // 128
+    per = tiles // 2
+    small = per // 2
+    big = per - small
+    wide = big * 128
+    full = width // 128 * 128
+    late = -(-4 * feat // 256) * 256
+    early = depth - late
+    a = rows_dev * 3 // 8 // 16 * 16
+    b = (rows_dev - a) // 32 * 16
+    spans = ((0, a), (a, b), (a + b, rows_dev - a - b))
+
+    clu, doc = lax.axis_index("clu"), lax.axis_index("doc")
+    core, chip = lax.rem(clu, 2), lax.div(clu, 2)
+    z, x = lax.div(chip, 2), lax.rem(chip, 2)
+    upper = z >= nz // 2
+
+    def device(r, dz=0):
+        dx, dy, dc = r // 4, r // 2 % 2, r % 2
+        there = ((z + dz) * 2 + (1 - x if dx else x)) * 2 + (1 - core if dc else core)
+        return {"clu": there, "doc": 1 - doc if dy else doc}
+
+    def when(cond, body):
+        if cond is None:
+            body()
+        else:
+            pl.when(cond)(body)
+
+    def both(p, q):
+        return q if p is None else p if q is None else p & q
+
+    sizes = ((None, big),) if big == small else ((1, big), (0, small))
+
+    def sized(c, cond, body):
+        for value, count in sizes:
+            when(both(cond, None if value is None else c == value), functools.partial(body, count * 128))
+
+    own_copy = pltpu.make_async_copy(cents_in.at[:, pl.ds(0, full)], own.at[:, pl.ds(0, full)], local_sem.at[0])
+    docs_copy = pltpu.make_async_copy(docs_in, docs.at[0], local_sem.at[1])
+    ids_copy = pltpu.make_async_copy(ids_in, ids.at[0], local_sem.at[2])
+    own_copy.start()
+    if full < width:
+        raw_copy = pltpu.make_async_copy(cents_in.at[:, pl.ds(full, width - full)], raw, local_sem.at[3])
+        raw_copy.start()
+    docs_copy.start()
+    ids_copy.start()
+
+    above, below = z < nz - 1, z > 0
+    barrier = pltpu.get_barrier_semaphore()
+
+    def greet(to):
+        pl.semaphore_signal(barrier, inc=1, device_id=to, device_id_type=MESH)
+
+    pl.when(above)(lambda: greet(device(0, 1)))
+    pl.when(below)(lambda: greet(device(0, -1)))
+    for r in (4, 5, 2, 1):
+        greet(device(r))
+    if small < big:
+        @pl.when(core == 0)
+        def _():
+            buf[:, pl.ds(small * 128, 128)] = jnp.zeros((buf.shape[0], 128), buf.dtype)
+    if full < width:
+        raw_copy.wait()
+        own[:, pl.ds(full, 128)] = jnp.concatenate(
+            [raw[...], jnp.zeros((feat, full + 128 - width), raw.dtype)], axis=1)
+    own_copy.wait()
+    docs_copy.wait()
+    ids_copy.wait()
+    pl.semaphore_wait(barrier, 4 + above.astype(jnp.int32) + below.astype(jnp.int32))
+
+    pending = []
+
+    def start(make, cond=None):
+        when(cond, lambda: make().start())
+        pending.append((cond, make))
+
+    def start_sized(make, c, cond=None):
+        sized(c, cond, lambda w: make(w).start())
+        pending.append((c, cond, make))
+
+    def remote(src, dst, ss, rs, to):
+        return pltpu.make_async_remote_copy(
+            src_ref=src, dst_ref=dst, send_sem=ss, recv_sem=rs, device_id=to, device_id_type=MESH)
+
+    near = (0, 1, 4, 5)
+
+    def source(layer, j):
+        r = near[j]
+        there = (layer * 2 + (1 - x if r // 4 else x)) * 2 + (1 - core if r % 2 else core)
+        return pl.ds(pl.multiple_of(there * feat, 16), feat)
+
+    def columns(r, w):
+        xd = 1 - x if r // 4 else x
+        cd = 1 - core if r % 2 else core
+        return pl.ds(pl.multiple_of((xd * per + cd * small) * 128, 128), w)
+
+    mine = source(z, 0)
+
+    def exchange(j):
+        r = near[j]
+        start_sized(lambda w: remote(own.at[:, columns(r, w)], buf.at[mine, pl.ds(0, w)],
+                                     c_send.at[j], c_recv.at[z, j], device(r)),
+                    1 - core if r % 2 else core)
+
+    def landed(layer, j, cond=None):
+        rows = source(layer, j)
+        sized(core, cond, lambda w: remote(
+            buf.at[rows, pl.ds(0, w)], buf.at[rows, pl.ds(0, w)], c_send.at[j], c_recv.at[layer, j],
+            device(1)).wait_recv())
+
+    def climb(layer, j, way, s, cond):
+        rows = source(layer, j)
+        src = (lambda w: own.at[:, columns(0, w)]) if s == 0 and j == 0 else (lambda w: buf.at[rows, pl.ds(0, w)])
+        start_sized(lambda w: remote(src(w), buf.at[rows, pl.ds(0, w)], z_send.at[way, s, j],
+                                     c_recv.at[layer, j], device(0, 1 - 2 * way)), core, cond)
+
+    def spread(j):
+        if j:
+            landed(z, j)
+        climb(z, j, 0, 0, above)
+        climb(z, j, 1, 0, below)
+
+    def relay(s, j):
+        up, down = z >= s, z + s < nz
+        landed(z - s, j, up)
+        if s < nz - 1:
+            climb(z - s, j, 0, s, up & above)
+        landed(z + s, j, down)
+        if s < nz - 1:
+            climb(z + s, j, 1, s, down & below)
+
+    def part(slot, p):
+        return docs.at[slot, pl.ds(*spans[p]), :]
+
+    def send_docs(src_slot, p, dst_slot, r):
+        start(lambda: remote(part(src_slot, p), part(dst_slot, p), d_send.at[dst_slot, p],
+                             d_recv.at[dst_slot, p], device(r)))
+
+    def send_ids(src_slot, dst_slot, r):
+        start(lambda: remote(ids.at[src_slot], ids.at[dst_slot], i_send.at[dst_slot],
+                             i_recv.at[dst_slot], device(r)))
+
+    def have_docs(slot, p):
+        remote(part(slot, p), part(slot, p), d_send.at[slot, p], d_recv.at[slot, p], device(1)).wait_recv()
+
+    def have_ids(slot):
+        remote(ids.at[slot], ids.at[slot], i_send.at[slot], i_recv.at[slot], device(1)).wait_recv()
+
+    def share(slot, p):
+        send_docs(slot, p, slot + 1, 1)
+
+    spread(0)
+    for j in (1, 2, 3):
+        exchange(j)
+    send_ids(0, 2, 2)
+    for p in (0, 1, 2):
+        send_docs(0, p, 2, 2)
+    send_ids(0, 4, 4)
+    for p in (1, 2, 0):
+        send_docs(0, p, 4, 4)
+    send_ids(0, 1, 1)
+    for p in (0, 1, 2):
+        send_docs(0, p, 1, 1)
+
+    part_cols = jnp.where(core == 1, big, small) * 128
+    first = (x * per + core * small) * 128
+    base = doc * width + first
+    reach = jnp.minimum(part_cols, width - first)
+    lanes = lax.broadcasted_iota(jnp.int32, (rows_dev, 128), 1)
+
+    def prepare_ids(slot):
+        rel = ids[slot] - base
+        rel = jnp.where((rel >= 0) & (rel < reach), rel, -1)
+        tall = jnp.broadcast_to(rel, (128, rows_dev)).T
+        idb[slot] = jnp.where(tall >= 0, tall - lanes, -(2**20))
+
+    buf[mine, pl.ds(0, small * 128)] = own[:, columns(0, small * 128)]
+    if small < big:
+        @pl.when(core == 1)
+        def _():
+            start_col = pl.multiple_of((x * per + 2 * small) * 128, 128)
+            buf[mine, pl.ds(small * 128, 128)] = own[:, pl.ds(start_col, 128)]
+
+    spread(1)
+    prepare_ids(0)
+    spread(2)
+    relay(1, 0)
+    spread(3)
+    relay(1, 1)
+    have_docs(2, 0)
+    send_docs(2, 0, 6, 4)
+    share(2, 0)
+    have_ids(4)
+    send_ids(4, 6, 2)
+    send_ids(4, 5, 1)
+    have_ids(2)
+    send_ids(2, 3, 1)
+    relay(1, 2)
+    have_docs(4, 1)
+    send_docs(4, 1, 6, 2)
+    share(4, 1)
+    relay(1, 3)
+    have_docs(2, 1)
+    share(2, 1)
+    for s in range(2, nz - 1):
+        relay(s, 0)
+    have_docs(4, 2)
+    send_docs(4, 2, 6, 2)
+    share(4, 2)
+    have_docs(2, 2)
+    share(2, 2)
+    have_ids(6)
+    send_ids(6, 7, 1)
+    for slot in (1, 2, 3, 4, 5, 6, 7):
+        if slot in (1, 3, 5, 7):
+            have_ids(slot)
+        prepare_ids(slot)
+    for s in range(2, nz - 1):
+        for j in (1, 2, 3):
+            relay(s, j)
+
+    early_at = pl.multiple_of(jnp.where(upper, late, 0), 256)
+    late_at = pl.multiple_of(jnp.where(upper, 0, early), 256)
+
+    def squares(at, count):
+        w32 = buf[pl.ds(at, count), :].astype(jnp.float32)
+        return jnp.sum((w32 * w32).reshape(count // 8, 8, wide), 0)
+
+    def begin(slot):
+        acc[slot] = jnp.dot(docs[slot, :, pl.ds(early_at, early)], buf[pl.ds(early_at, early), :],
+                            preferred_element_type=jnp.float32)
+
+    csq[...] = squares(early_at, early)
+    begin(0)
+    for p in (0, 1, 2):
+        have_docs(1, p)
+    begin(1)
+    begin(2)
+    have_docs(4, 0)
+    share(4, 0)
+    for p in (0, 1, 2):
+        have_docs(3, p)
+    begin(3)
+    begin(4)
+    for p in (1, 2, 0):
+        have_docs(6, p)
+        share(6, p)
+    for p in (1, 2, 0):
+        have_docs(5, p)
+    begin(5)
+    begin(6)
+    for p in (1, 2, 0):
+        have_docs(7, p)
+    begin(7)
+    for j in (0, 1, 2, 3):
+        relay(nz - 1, j)
+
+    total = jnp.sum(csq[...] + squares(late_at, late), 0, keepdims=True)
+    scale[...] = lax.rsqrt(total + epsilon)
+    lane = lax.broadcasted_iota(jnp.int32, (1, 128), 1)
+
+    def finish(slot):
+        prod = jnp.dot(docs[slot, :, pl.ds(late_at, late)], buf[pl.ds(late_at, late), :],
+                       preferred_element_type=jnp.float32)
+        tops, hits = [], []
+        for r in range(0, rows_dev, ROWS):
+            rs = pl.ds(r, ROWS)
+            top = jnp.full((ROWS, 128), -3.0e38, jnp.float32)
+            hit = jnp.zeros((ROWS, 128), jnp.float32)
+            where_id = idb[slot, rs, :]
+            for c in range(0, wide, 128):
+                cols = pl.ds(c, 128)
+                v = (acc[slot, rs, cols] + prod[r:r + ROWS, c:c + 128]) * scale[:, cols]
+                hit = jnp.where(where_id == c, v, hit)
+                if c + 128 > small * 128 or (c + 128 == small * 128 and small == big):
+                    v = jnp.where(lane < reach - c, v, -3.0e38)
+                top = jnp.maximum(top, v)
+            tops.append(top)
+            hits.append(hit)
+        return (jnp.max(jnp.concatenate(tops, 0).T, 0, keepdims=True),
+                jnp.sum(jnp.concatenate(hits, 0).T, 0, keepdims=True))
+
+    for slot in (7, 6, 3, 2, 5, 4, 1):
+        best, chosen = finish(slot)
+        res[slot, 0:1, :] = best
+        res[slot, 1:2, :] = chosen
+        start(lambda slot=slot: remote(res.at[slot], got.at[slot], r_send.at[slot], r_recv.at[slot], device(slot)))
+    best, chosen = finish(0)
+    x32 = docs[0].astype(jnp.float32)
+    sq = x32 * x32
+    total = sq[:, 0:128]
+    for c in range(128, depth, 128):
+        total = total + sq[:, c:c + 128]
+    scale_x = lax.rsqrt(jnp.sum(total.T, 0, keepdims=True) + epsilon)
+    for slot in (1, 4, 5, 2, 3, 6, 7):
+        remote(res.at[slot], got.at[slot], r_send.at[slot], r_recv.at[slot], device(slot)).wait_recv()
+        best = jnp.maximum(best, got[slot, 0:1, :])
+        chosen = chosen + got[slot, 1:2, :]
+    near_out[...] = best * scale_x
+    chosen_out[...] = chosen * scale_x
+    for entry in pending:
+        if len(entry) == 2:
+            cond, make = entry
+            when(cond, lambda: make().wait_send())
+        else:
+            c, cond, make = entry
+            sized(c, cond, lambda w: make(w).wait_send())
+
+
+def by_layers(docs, centroids, assigned):
+    nz = lax.axis_size("clu") // 4
+    rows_dev, depth = docs.shape
+    width, feat = centroids.shape
+    tiles = -(-width // 128)
+    wide = (tiles // 2 - tiles // 4) * 128
+    any_space = pl.BlockSpec(memory_space=pl.ANY)
+    vmem = pl.BlockSpec(memory_space=pltpu.VMEM)
+    dma = pltpu.SemaphoreType.DMA
+    line = jax.ShapeDtypeStruct((1, rows_dev), jnp.float32)
+    near, chosen = pl.pallas_call(
+        functools.partial(layer_kernel, nz, feat),
+        out_shape=(line, line),
+        in_specs=[any_space] * 3,
+        out_specs=(vmem, vmem),
+        scratch_shapes=[
+            pltpu.VMEM((feat, tiles * 128), jnp.bfloat16),
+            pltpu.VMEM((feat, width % 128 or 128), jnp.bfloat16),
+            pltpu.VMEM((depth, wide), jnp.bfloat16),
+            pltpu.VMEM((8, rows_dev, depth), jnp.bfloat16),
+            pltpu.VMEM((8, 1, rows_dev), jnp.int32),
+            pltpu.VMEM((8, rows_dev, wide), jnp.float32),
+            pltpu.VMEM((8, rows_dev, 128), jnp.int32),
+            pltpu.VMEM((8, wide), jnp.float32),
+            pltpu.VMEM((1, wide), jnp.float32),
+            pltpu.VMEM((8, 2, rows_dev), jnp.float32),
+            pltpu.VMEM((8, 2, rows_dev), jnp.float32),
+            dma((4,)),
+            dma((4,)), dma((nz, 4)), dma((2, nz, 4)),
+            dma((8, 3)), dma((8, 3)), dma((8,)), dma((8,)), dma((8,)), dma((8,)),
+        ],
+        compiler_params=pltpu.CompilerParams(collective_id=0, has_side_effects=True),
+        name="layer_distances",
+    )(docs, centroids.T, assigned.reshape(1, rows_dev))
+    return 1.0 - near.reshape(rows_dev), 1.0 - chosen.reshape(rows_dev)
+
+
+def fits_layers(docs, centroids):
+    tiles = -(-centroids.shape[0] // 128)
+    n_clu, feat = lax.axis_size("clu"), centroids.shape[1]
+    return (lax.axis_size("doc") == 2 and n_clu % 8 == 0 and tiles % 2 == 0 and tiles >= 4
+            and feat % 16 == 0 and docs.shape[0] % 128 == 0 and docs.shape[1] % 256 == 0
+            and docs.shape[1] > 4 * feat + 255)
+
+
 def on_device(docs, centroids, assigned):
+    if fits_layers(docs, centroids):
+        return by_layers(docs, centroids, assigned)
     n_clu, nd = lax.axis_size("clu"), lax.axis_size("doc")
     n = n_clu // 2
     rows_dev, depth = docs.shape

time: 34.6 us -> 31.9 us (0.922)
  Pallas kernels: 32.6 us -> 29.9 us
    pallas_call x1, Pallas kernels: 32.6 us -> 29.9 us  [by_layers(): pl.pallas_call(functools.partial(layer_kernel, nz, feat), out_shape=(line...]
where the time goes in v1:
time: 31.9 us; the launch traced here: 31.7 us
  Pallas kernels  29.9 us (94%)
  between operations  0.65 us (2%)
  local copies, waits for them, and re-layouts  0.63 us (2%)
  other arithmetic  0.57 us (2%)
    pallas_call x1, Pallas kernels, by_layers(): pl.pallas_call(functools.partial(layer_kernel, nz, feat), out_shape=(line...  29.9 us

profile of v1, /device:TPU:0, one launch (start us, length us, event | category | flops | bytes accessed | tf_op | source)
XLA Modules:
  0.0 31.7 jit_solution(9935046350275266401)
XLA Ops:
  0.6 29.9 %layer_distances.1 = (f32[1,256]{1,0:T(1,128)}, f32[1,256]{1,0:T(1,128)}) custom-call(bf16[256,768]{1,0:T(8,128)(2,1)} %docs_in.1, bf16[48,2752]{1,0:T(8,128)(2,1)} %bitcast.4, s32[1,256]{1,0:T(1,128)} %bitcast.5), custom_call_target="tpu_custom_call" | custom-call | tf_op jit(solution)/shard_map/layer_distances/pallas_call | solution.py:617
  30.5 0.0 copy-start.1
  30.5 0.0 copy-start
  30.5 0.6 %copy-done.1 = f32[1,256]{1,0:T(1,128)S(1)} copy-done((f32[1,256]{1,0:T(1,128)S(1)}, f32[1,256]{1,0:T(1,128)}, u32[]{:S(2)}) %copy-start.1) | copy-done | bytes 1048
  31.1 0.0 copy-done
  31.1 0.6 %broadcast_subtract_fusion = (f32[1,256]{1,0:T(1,128)}, f32[1,256]{1,0:T(1,128)}) fusion(f32[1,256]{1,0:T(1,128)S(1)} %copy-done.1, f32[1,256]{1,0:T(1,128)S(1)} %copy-done), kind=kLoop, calls=%fused_computation | loop fusion | flops 512 | bytes 4096 | tf_op jit(solution)/shard_map/sub | solution.py:641
Async XLA Ops:
  30.5 0.6 %copy-start.1 = (f32[1,256]{1,0:T(1,128)S(1)}, f32[1,256]{1,0:T(1,128)}, u32[]{:S(2)}) copy-start(f32[1,256]{1,0:T(1,128)} %get-tuple-element.5) | copy-start | bytes 3076
  30.5 0.6 %copy-start = (f32[1,256]{1,0:T(1,128)S(1)}, f32[1,256]{1,0:T(1,128)}, u32[]{:S(2)}) copy-start(f32[1,256]{1,0:T(1,128)} %get-tuple-element.4) | copy-start | bytes 3076

commit v2 on v1

--- a/solution.py
+++ b/solution.py
@@ -291,8 +291,9 @@
 
 
 def layer_kernel(nz, feat, docs_in, cents_in, ids_in, near_out, chosen_out,
-                 own, raw, buf, docs, ids, acc, idb, csq, scale, res, got,
-                 local_sem, c_send, c_recv, z_send, d_send, d_recv, i_send, i_recv, r_send, r_recv):
+                 own, raw, buf, docs, ids, acc, idb, mx, ch, csq, scale, res, got,
+                 local_sem, c_send, c_recv, z_send, last_send, last_recv,
+                 d_send, d_recv, i_send, i_recv, r_send, r_recv):
     width = cents_in.shape[1]
     rows_dev, depth = docs_in.shape
     tiles = own.shape[1] // 128
@@ -302,15 +303,20 @@
     wide = big * 128
     full = width // 128 * 128
     late = -(-4 * feat // 256) * 256
-    early = depth - late
-    a = rows_dev * 3 // 8 // 16 * 16
+    k1 = 8 * feat // 256 * 256
+    k2 = depth - late - k1
+    a = rows_dev * 5 // 16 // 16 * 16
     b = (rows_dev - a) // 32 * 16
     spans = ((0, a), (a, b), (a + b, rows_dev - a - b))
+    chunks = tuple((c, min(256, wide - c)) for c in range(0, wide, 256))
 
     clu, doc = lax.axis_index("clu"), lax.axis_index("doc")
     core, chip = lax.rem(clu, 2), lax.div(clu, 2)
     z, x = lax.div(chip, 2), lax.rem(chip, 2)
     upper = z >= nz // 2
+    out = jnp.where(upper, 1, -1)
+    end = (z == 0) | (z == nz - 1)
+    inner = jnp.logical_not(end)
 
     def device(r, dz=0):
         dx, dy, dc = r // 4, r // 2 % 2, r % 2
@@ -342,14 +348,13 @@
     docs_copy.start()
     ids_copy.start()
 
-    above, below = z < nz - 1, z > 0
     barrier = pltpu.get_barrier_semaphore()
 
     def greet(to):
         pl.semaphore_signal(barrier, inc=1, device_id=to, device_id_type=MESH)
 
-    pl.when(above)(lambda: greet(device(0, 1)))
-    pl.when(below)(lambda: greet(device(0, -1)))
+    pl.when(inner)(lambda: greet(device(0, out)))
+    greet(device(0, -out))
     for r in (4, 5, 2, 1):
         greet(device(r))
     if small < big:
@@ -363,7 +368,7 @@
     own_copy.wait()
     docs_copy.wait()
     ids_copy.wait()
-    pl.semaphore_wait(barrier, 4 + above.astype(jnp.int32) + below.astype(jnp.int32))
+    pl.semaphore_wait(barrier, 5 + inner.astype(jnp.int32))
 
     pending = []
 
@@ -405,26 +410,43 @@
             buf.at[rows, pl.ds(0, w)], buf.at[rows, pl.ds(0, w)], c_send.at[j], c_recv.at[layer, j],
             device(1)).wait_recv())
 
-    def climb(layer, j, way, s, cond):
+    def carry(layer, j, way, s, cond=None):
         rows = source(layer, j)
         src = (lambda w: own.at[:, columns(0, w)]) if s == 0 and j == 0 else (lambda w: buf.at[rows, pl.ds(0, w)])
         start_sized(lambda w: remote(src(w), buf.at[rows, pl.ds(0, w)], z_send.at[way, s, j],
-                                     c_recv.at[layer, j], device(0, 1 - 2 * way)), core, cond)
+                                     c_recv.at[layer, j], device(0, -out if way else out)), core, cond)
 
     def spread(j):
         if j:
             landed(z, j)
-        climb(z, j, 0, 0, above)
-        climb(z, j, 1, 0, below)
-
-    def relay(s, j):
-        up, down = z >= s, z + s < nz
-        landed(z - s, j, up)
-        if s < nz - 1:
-            climb(z - s, j, 0, s, up & above)
-        landed(z + s, j, down)
-        if s < nz - 1:
-            climb(z + s, j, 1, s, down & below)
+        carry(z, j, 0, 0, inner)
+        carry(z, j, 1, 0)
+
+    def relay(j):
+        landed(z - out, j)
+        carry(z - out, j, 0, 1, inner)
+        landed(z + out, j, inner)
+        carry(z + out, j, 1, 1, inner)
+
+    def pair(layer, k, w):
+        rows = pl.ds(pl.multiple_of((layer * 2 + 1 - x) * 2 * feat, 16), 2 * feat)
+        c = chunks[k][0]
+        return buf.at[rows, pl.ds(c, min(w, c + chunks[k][1]) - c)]
+
+    def relay_far(j):
+        landed(z - 2 * out, j)
+        if j < 2:
+            carry(z - 2 * out, j, 0, 2, inner)
+        elif j == 3:
+            for k in range(len(chunks)):
+                start_sized(lambda w, k=k: remote(
+                    pair(z - 2 * out, k, w), pair(z - 2 * out, k, w), last_send.at[k], last_recv.at[k],
+                    device(0, out)), core, inner)
+
+    def last_landed(k):
+        sized(core, end, lambda w: remote(
+            pair(z - 3 * out, k, w), pair(z - 3 * out, k, w), last_send.at[k], last_recv.at[k],
+            device(1)).wait_recv())
 
     def part(slot, p):
         return docs.at[slot, pl.ds(*spans[p]), :]
@@ -437,8 +459,9 @@
         start(lambda: remote(ids.at[src_slot], ids.at[dst_slot], i_send.at[dst_slot],
                              i_recv.at[dst_slot], device(r)))
 
-    def have_docs(slot, p):
-        remote(part(slot, p), part(slot, p), d_send.at[slot, p], d_recv.at[slot, p], device(1)).wait_recv()
+    def have_docs(slot, *parts):
+        for p in parts:
+            remote(part(slot, p), part(slot, p), d_send.at[slot, p], d_recv.at[slot, p], device(1)).wait_recv()
 
     def have_ids(slot):
         remote(ids.at[slot], ids.at[slot], i_send.at[slot], i_recv.at[slot], device(1)).wait_recv()
@@ -464,6 +487,7 @@
     base = doc * width + first
     reach = jnp.minimum(part_cols, width - first)
     lanes = lax.broadcasted_iota(jnp.int32, (rows_dev, 128), 1)
+    lane = lax.broadcasted_iota(jnp.int32, (1, 128), 1)
 
     def prepare_ids(slot):
         rel = ids[slot] - base
@@ -478,12 +502,30 @@
             start_col = pl.multiple_of((x * per + 2 * small) * 128, 128)
             buf[mine, pl.ds(small * 128, 128)] = own[:, pl.ds(start_col, 128)]
 
+    k1_at = pl.multiple_of(jnp.where(upper, depth - k1, 0), 256)
+    k2_at = pl.multiple_of(jnp.where(upper, late, k1), 256)
+    early_at = pl.multiple_of(jnp.where(upper, late, 0), 256)
+    late_at = pl.multiple_of(jnp.where(upper, 0, depth - late), 256)
+
+    def squares(at, count, c, w):
+        w32 = buf[pl.ds(at, count), pl.ds(c, w)].astype(jnp.float32)
+        return jnp.sum((w32 * w32).reshape(count // 8, 8, w), 0)
+
+    def begin(slot, count, at, deep, add=False):
+        rows = docs[pl.ds(slot, count), :, pl.ds(at, deep)].reshape(count * rows_dev, deep)
+        prod = jnp.dot(rows, buf[pl.ds(at, deep), :], preferred_element_type=jnp.float32)
+        prod = prod.reshape(count, rows_dev, wide)
+        if add:
+            acc[pl.ds(slot, count)] += prod
+        else:
+            acc[pl.ds(slot, count)] = prod
+
     spread(1)
     prepare_ids(0)
     spread(2)
-    relay(1, 0)
+    relay(0)
     spread(3)
-    relay(1, 1)
+    relay(1)
     have_docs(2, 0)
     send_docs(2, 0, 6, 4)
     share(2, 0)
@@ -492,15 +534,14 @@
     send_ids(4, 5, 1)
     have_ids(2)
     send_ids(2, 3, 1)
-    relay(1, 2)
+    relay(2)
     have_docs(4, 1)
     send_docs(4, 1, 6, 2)
     share(4, 1)
-    relay(1, 3)
     have_docs(2, 1)
     share(2, 1)
-    for s in range(2, nz - 1):
-        relay(s, 0)
+    relay(3)
+    relay_far(0)
     have_docs(4, 2)
     send_docs(4, 2, 6, 2)
     share(4, 2)
@@ -508,81 +549,94 @@
     share(2, 2)
     have_ids(6)
     send_ids(6, 7, 1)
+    have_docs(1, 0, 1, 2)
+    begin(0, 2, k1_at, k1)
+    relay_far(1)
     for slot in (1, 2, 3, 4, 5, 6, 7):
         if slot in (1, 3, 5, 7):
             have_ids(slot)
         prepare_ids(slot)
-    for s in range(2, nz - 1):
-        for j in (1, 2, 3):
-            relay(s, j)
-
-    early_at = pl.multiple_of(jnp.where(upper, late, 0), 256)
-    late_at = pl.multiple_of(jnp.where(upper, 0, early), 256)
-
-    def squares(at, count):
-        w32 = buf[pl.ds(at, count), :].astype(jnp.float32)
-        return jnp.sum((w32 * w32).reshape(count // 8, 8, wide), 0)
-
-    def begin(slot):
-        acc[slot] = jnp.dot(docs[slot, :, pl.ds(early_at, early)], buf[pl.ds(early_at, early), :],
-                            preferred_element_type=jnp.float32)
-
-    csq[...] = squares(early_at, early)
-    begin(0)
-    for p in (0, 1, 2):
-        have_docs(1, p)
-    begin(1)
-    begin(2)
     have_docs(4, 0)
     share(4, 0)
-    for p in (0, 1, 2):
-        have_docs(3, p)
-    begin(3)
-    begin(4)
+    relay_far(2)
+    have_docs(3, 0, 1, 2)
+    begin(2, 2, k1_at, k1)
+    csq[...] = squares(k1_at, k1, 0, wide)
+    relay_far(3)
+    begin(0, 2, k2_at, k2, True)
+    begin(2, 2, k2_at, k2, True)
+    csq[...] += squares(k2_at, k2, 0, wide)
+    have_docs(5, 1, 2, 0)
+    begin(4, 2, early_at, k1 + k2)
     for p in (1, 2, 0):
         have_docs(6, p)
         share(6, p)
-    for p in (1, 2, 0):
-        have_docs(5, p)
-    begin(5)
-    begin(6)
-    for p in (1, 2, 0):
-        have_docs(7, p)
-    begin(7)
-    for j in (0, 1, 2, 3):
-        relay(nz - 1, j)
-
-    total = jnp.sum(csq[...] + squares(late_at, late), 0, keepdims=True)
-    scale[...] = lax.rsqrt(total + epsilon)
-    lane = lax.broadcasted_iota(jnp.int32, (1, 128), 1)
-
-    def finish(slot):
-        prod = jnp.dot(docs[slot, :, pl.ds(late_at, late)], buf[pl.ds(late_at, late), :],
-                       preferred_element_type=jnp.float32)
-        tops, hits = [], []
-        for r in range(0, rows_dev, ROWS):
-            rs = pl.ds(r, ROWS)
-            top = jnp.full((ROWS, 128), -3.0e38, jnp.float32)
-            hit = jnp.zeros((ROWS, 128), jnp.float32)
-            where_id = idb[slot, rs, :]
-            for c in range(0, wide, 128):
-                cols = pl.ds(c, 128)
-                v = (acc[slot, rs, cols] + prod[r:r + ROWS, c:c + 128]) * scale[:, cols]
-                hit = jnp.where(where_id == c, v, hit)
-                if c + 128 > small * 128 or (c + 128 == small * 128 and small == big):
-                    v = jnp.where(lane < reach - c, v, -3.0e38)
-                top = jnp.maximum(top, v)
-            tops.append(top)
-            hits.append(hit)
-        return (jnp.max(jnp.concatenate(tops, 0).T, 0, keepdims=True),
-                jnp.sum(jnp.concatenate(hits, 0).T, 0, keepdims=True))
-
-    for slot in (7, 6, 3, 2, 5, 4, 1):
-        best, chosen = finish(slot)
+    begin(6, 1, early_at, k1 + k2)
+
+    def scales(k):
+        c, w = chunks[k]
+        total = jnp.sum(csq[:, pl.ds(c, w)] + squares(late_at, late, c, w), 0, keepdims=True)
+        scale[:, pl.ds(c, w)] = lax.rsqrt(total + epsilon)
+
+    def stage(k, slot):
+        c0, w = chunks[k]
+        rows = docs[pl.ds(slot, 2), :, pl.ds(late_at, late)].reshape(2 * rows_dev, late)
+        prod = jnp.dot(rows, buf[pl.ds(late_at, late), pl.ds(c0, w)], preferred_element_type=jnp.float32)
+        for half in (0, 1):
+            for r in range(0, rows_dev, ROWS):
+                rs = pl.ds(r, ROWS)
+                at = half * rows_dev + r
+                if k:
+                    top, hit = mx[slot + half, rs, :], ch[slot + half, rs, :]
+                else:
+                    top = jnp.full((ROWS, 128), -3.0e38, jnp.float32)
+                    hit = jnp.zeros((ROWS, 128), jnp.float32)
+                where_id = idb[slot + half, rs, :]
+                for c in range(0, w, 128):
+                    cols = pl.ds(c0 + c, 128)
+                    v = (acc[slot + half, rs, cols] + prod[at:at + ROWS, c:c + 128]) * scale[:, cols]
+                    hit = jnp.where(where_id == c0 + c, v, hit)
+                    if c0 + c + 128 > small * 128 or (c0 + c + 128 == small * 128 and small == big):
+                        v = jnp.where(lane < reach - (c0 + c), v, -3.0e38)
+                    top = jnp.maximum(top, v)
+                mx[slot + half, rs, :] = top
+                ch[slot + half, rs, :] = hit
+
+    def reduced(slot):
+        return (jnp.max(mx[slot].T, 0, keepdims=True), jnp.sum(ch[slot].T, 0, keepdims=True))
+
+    def give(slot):
+        best, chosen = reduced(slot)
         res[slot, 0:1, :] = best
         res[slot, 1:2, :] = chosen
-        start(lambda slot=slot: remote(res.at[slot], got.at[slot], r_send.at[slot], r_recv.at[slot], device(slot)))
-    best, chosen = finish(0)
+        start(lambda: remote(res.at[slot], got.at[slot], r_send.at[slot], r_recv.at[slot], device(slot)))
+
+    landed(z - 3 * out, 0, end)
+    landed(z - 3 * out, 1, end)
+    final = len(chunks) - 1
+    for k in range(final):
+        last_landed(k)
+        scales(k)
+        for slot in (0, 2, 4):
+            stage(k, slot)
+        if k == 0:
+            have_docs(7, 1, 2, 0)
+            begin(7, 1, early_at, k1 + k2)
+        stage(k, 6)
+    last_landed(final)
+    scales(final)
+    stage(final, 6)
+    stage(final, 2)
+    give(7)
+    give(6)
+    stage(final, 4)
+    give(3)
+    give(2)
+    stage(final, 0)
+    give(5)
+    give(4)
+    give(1)
+    best, chosen = reduced(0)
     x32 = docs[0].astype(jnp.float32)
     sq = x32 * x32
     total = sq[:, 0:128]
@@ -613,7 +667,7 @@
     any_space = pl.BlockSpec(memory_space=pl.ANY)
     vmem = pl.BlockSpec(memory_space=pltpu.VMEM)
     dma = pltpu.SemaphoreType.DMA
-    line = jax.ShapeDtypeStruct((1, rows_dev), jnp.float32)
+    line = pltpu.VMEM((1, rows_dev), jnp.float32)
     near, chosen = pl.pallas_call(
         functools.partial(layer_kernel, nz, feat),
         out_shape=(line, line),
@@ -627,12 +681,14 @@
             pltpu.VMEM((8, 1, rows_dev), jnp.int32),
             pltpu.VMEM((8, rows_dev, wide), jnp.float32),
             pltpu.VMEM((8, rows_dev, 128), jnp.int32),
+            pltpu.VMEM((8, rows_dev, 128), jnp.float32),
+            pltpu.VMEM((8, rows_dev, 128), jnp.float32),
             pltpu.VMEM((8, wide), jnp.float32),
             pltpu.VMEM((1, wide), jnp.float32),
             pltpu.VMEM((8, 2, rows_dev), jnp.float32),
             pltpu.VMEM((8, 2, rows_dev), jnp.float32),
             dma((4,)),
-            dma((4,)), dma((nz, 4)), dma((2, nz, 4)),
+            dma((4,)), dma((nz, 4)), dma((2, 3, 4)), dma((-(-wide // 256),)), dma((-(-wide // 256),)),
             dma((8, 3)), dma((8, 3)), dma((8,)), dma((8,)), dma((8,)), dma((8,)),
         ],
         compiler_params=pltpu.CompilerParams(collective_id=0, has_side_effects=True),
@@ -644,9 +700,9 @@
 def fits_layers(docs, centroids):
     tiles = -(-centroids.shape[0] // 128)
     n_clu, feat = lax.axis_size("clu"), centroids.shape[1]
-    return (lax.axis_size("doc") == 2 and n_clu % 8 == 0 and tiles % 2 == 0 and tiles >= 4
+    return (lax.axis_size("doc") == 2 and n_clu == 16 and tiles % 2 == 0 and tiles >= 4
             and feat % 16 == 0 and docs.shape[0] % 128 == 0 and docs.shape[1] % 256 == 0
-            and docs.shape[1] > 4 * feat + 255)
+            and docs.shape[1] == n_clu * feat and 8 * feat >= 256)
 
 
 def on_device(docs, centroids, assigned):

time: 31.9 us -> 30.4 us (0.953)
  Pallas kernels: 29.9 us -> 29 us
  local copies, waits for them, and re-layouts: 0.63 us -> 0 us
    pallas_call x1, Pallas kernels: 29.9 us -> 29 us  [by_layers(): pl.pallas_call(functools.partial(layer_kernel, nz, feat), out_shape=(line...]
    unnamed x4 -> x0, local copies, waits for them, and re-layouts: 0.63 us -> none
where the time goes in v2:
time: 30.4 us; the launch traced here: 30.2 us
  Pallas kernels  29 us (95%)
  between operations  0.64 us (2%)
  other arithmetic  0.57 us (2%)
    pallas_call x1, Pallas kernels, by_layers(): pl.pallas_call(functools.partial(layer_kernel, nz, feat), out_shape=(line...  29 us

profile of v2, /device:TPU:0, one launch (start us, length us, event | category | flops | bytes accessed | tf_op | source)
XLA Modules:
  0.0 30.2 jit_solution(3050755394835432994)
XLA Ops:
  0.6 29.0 %layer_distances.1 = (f32[1,256]{1,0:T(1,128)S(1)}, f32[1,256]{1,0:T(1,128)S(1)}) custom-call(bf16[256,768]{1,0:T(8,128)(2,1)} %docs_in.1, bf16[48,2752]{1,0:T(8,128)(2,1)} %bitcast.4, s32[1,256]{1,0:T(1,128)} %bitcast.5), custom_call_target="tpu_custom_call" | custom-call | tf_op jit(solution)/shard_map/layer_distances/pallas_call | solution.py:671
  29.7 0.6 %broadcast_subtract_fusion = (f32[1,256]{1,0:T(1,128)}, f32[1,256]{1,0:T(1,128)}) fusion(f32[1,256]{1,0:T(1,128)S(1)} %get-tuple-element.5, f32[1,256]{1,0:T(1,128)S(1)} %get-tuple-element.4), kind=kLoop, calls=%fused_computation | loop fusion | flops 512 | bytes 4096 | tf_op jit(solution)/shard_map/sub | solution.py:697

commit v3 on v2

--- a/solution.py
+++ b/solution.py
@@ -10,6 +10,7 @@
 epsilon = 1e-06
 PIECES = 4
 ROWS = 64
+GROUP = 32
 MESH = pl.DeviceIdType.MESH
 
 
@@ -291,9 +292,8 @@
 
 
 def layer_kernel(nz, feat, docs_in, cents_in, ids_in, near_out, chosen_out,
-                 own, raw, buf, docs, ids, acc, idb, mx, ch, csq, scale, res, got,
-                 local_sem, c_send, c_recv, z_send, last_send, last_recv,
-                 d_send, d_recv, i_send, i_recv, r_send, r_recv):
+                 own, raw, buf, docs, ids, turned, acc, idb, mx, ch, csq, scale, res, got,
+                 local_sem, send_sem, c_recv, last_recv, d_recv, i_recv, r_recv):
     width = cents_in.shape[1]
     rows_dev, depth = docs_in.shape
     tiles = own.shape[1] // 128
@@ -370,15 +370,13 @@
     ids_copy.wait()
     pl.semaphore_wait(barrier, 5 + inner.astype(jnp.int32))
 
-    pending = []
+    outward, inward, traded, doc_sent, id_sent, result_sent = (send_sem.at[i] for i in range(6))
 
     def start(make, cond=None):
         when(cond, lambda: make().start())
-        pending.append((cond, make))
 
     def start_sized(make, c, cond=None):
         sized(c, cond, lambda w: make(w).start())
-        pending.append((c, cond, make))
 
     def remote(src, dst, ss, rs, to):
         return pltpu.make_async_remote_copy(
@@ -401,19 +399,19 @@
     def exchange(j):
         r = near[j]
         start_sized(lambda w: remote(own.at[:, columns(r, w)], buf.at[mine, pl.ds(0, w)],
-                                     c_send.at[j], c_recv.at[z, j], device(r)),
+                                     traded, c_recv.at[z, j], device(r)),
                     1 - core if r % 2 else core)
 
     def landed(layer, j, cond=None):
         rows = source(layer, j)
         sized(core, cond, lambda w: remote(
-            buf.at[rows, pl.ds(0, w)], buf.at[rows, pl.ds(0, w)], c_send.at[j], c_recv.at[layer, j],
+            buf.at[rows, pl.ds(0, w)], buf.at[rows, pl.ds(0, w)], traded, c_recv.at[layer, j],
             device(1)).wait_recv())
 
     def carry(layer, j, way, s, cond=None):
         rows = source(layer, j)
         src = (lambda w: own.at[:, columns(0, w)]) if s == 0 and j == 0 else (lambda w: buf.at[rows, pl.ds(0, w)])
-        start_sized(lambda w: remote(src(w), buf.at[rows, pl.ds(0, w)], z_send.at[way, s, j],
+        start_sized(lambda w: remote(src(w), buf.at[rows, pl.ds(0, w)], inward if way else outward,
                                      c_recv.at[layer, j], device(0, -out if way else out)), core, cond)
 
     def spread(j):
@@ -440,60 +438,64 @@
         elif j == 3:
             for k in range(len(chunks)):
                 start_sized(lambda w, k=k: remote(
-                    pair(z - 2 * out, k, w), pair(z - 2 * out, k, w), last_send.at[k], last_recv.at[k],
+                    pair(z - 2 * out, k, w), pair(z - 2 * out, k, w), outward, last_recv.at[k],
                     device(0, out)), core, inner)
 
     def last_landed(k):
         sized(core, end, lambda w: remote(
-            pair(z - 3 * out, k, w), pair(z - 3 * out, k, w), last_send.at[k], last_recv.at[k],
+            pair(z - 3 * out, k, w), pair(z - 3 * out, k, w), outward, last_recv.at[k],
             device(1)).wait_recv())
 
-    def part(slot, p):
-        return docs.at[slot, pl.ds(*spans[p]), :]
-
-    def send_docs(src_slot, p, dst_slot, r):
-        start(lambda: remote(part(src_slot, p), part(dst_slot, p), d_send.at[dst_slot, p],
-                             d_recv.at[dst_slot, p], device(r)))
+    ahead = {(1, 0): 0, (1, 1): 0, (1, 2): 0, (3, 0): 1, (3, 1): 1, (3, 2): 1, (5, 0): 2, (5, 1): 2, (5, 2): 2,
+             (7, 0): 3, (7, 1): 3, (7, 2): 3, (2, 0): 4, (2, 1): 5, (2, 2): 5, (4, 0): 6, (4, 1): 7, (4, 2): 8,
+             (6, 0): 9, (6, 1): 10, (6, 2): 11}
+    id_at = {1: 0, 3: 0, 5: 0, 7: 0, 2: 1, 4: 2, 6: 3}
+
+    def part(slot, *parts):
+        first, last = spans[parts[0]], spans[parts[-1]]
+        return docs.at[slot, pl.ds(first[0], last[0] + last[1] - first[0]), :]
+
+    def send_docs(src_slot, dst_slot, r, *parts):
+        start(lambda: remote(part(src_slot, *parts), part(dst_slot, *parts), doc_sent,
+                             d_recv.at[ahead[dst_slot, parts[0]]], device(r)))
 
     def send_ids(src_slot, dst_slot, r):
-        start(lambda: remote(ids.at[src_slot], ids.at[dst_slot], i_send.at[dst_slot],
-                             i_recv.at[dst_slot], device(r)))
+        start(lambda: remote(ids.at[src_slot], ids.at[dst_slot], id_sent, i_recv.at[id_at[dst_slot]], device(r)))
 
     def have_docs(slot, *parts):
-        for p in parts:
-            remote(part(slot, p), part(slot, p), d_send.at[slot, p], d_recv.at[slot, p], device(1)).wait_recv()
+        remote(part(slot, *parts), part(slot, *parts), doc_sent, d_recv.at[ahead[slot, parts[0]]],
+               device(1)).wait_recv()
 
     def have_ids(slot):
-        remote(ids.at[slot], ids.at[slot], i_send.at[slot], i_recv.at[slot], device(1)).wait_recv()
-
-    def share(slot, p):
-        send_docs(slot, p, slot + 1, 1)
+        some = ids.at[pl.ds(0, 4)] if slot % 2 else ids.at[slot]
+        remote(some, some, id_sent, i_recv.at[id_at[slot]], device(1)).wait_recv()
+
+    def share(slot, *parts):
+        send_docs(slot, slot + 1, 1, *parts)
 
     spread(0)
     for j in (1, 2, 3):
         exchange(j)
     send_ids(0, 2, 2)
-    for p in (0, 1, 2):
-        send_docs(0, p, 2, 2)
+    send_docs(0, 2, 2, 0)
+    send_docs(0, 2, 2, 1, 2)
     send_ids(0, 4, 4)
     for p in (1, 2, 0):
-        send_docs(0, p, 4, 4)
+        send_docs(0, 4, 4, p)
     send_ids(0, 1, 1)
-    for p in (0, 1, 2):
-        send_docs(0, p, 1, 1)
+    send_docs(0, 1, 1, 0, 1, 2)
 
     part_cols = jnp.where(core == 1, big, small) * 128
     first = (x * per + core * small) * 128
     base = doc * width + first
     reach = jnp.minimum(part_cols, width - first)
-    lanes = lax.broadcasted_iota(jnp.int32, (rows_dev, 128), 1)
-    lane = lax.broadcasted_iota(jnp.int32, (1, 128), 1)
+    down = lax.broadcasted_iota(jnp.int32, (GROUP, 128), 0)
 
     def prepare_ids(slot):
         rel = ids[slot] - base
-        rel = jnp.where((rel >= 0) & (rel < reach), rel, -1)
-        tall = jnp.broadcast_to(rel, (128, rows_dev)).T
-        idb[slot] = jnp.where(tall >= 0, tall - lanes, -(2**20))
+        rel = jnp.where((rel >= 0) & (rel < reach), rel, -(2**20))
+        tall = jnp.broadcast_to(rel, (GROUP, rows_dev))
+        idb[:, pl.ds(slot * rows_dev, rows_dev)] = tall - lax.broadcasted_iota(jnp.int32, (GROUP, rows_dev), 0)
 
     buf[mine, pl.ds(0, small * 128)] = own[:, columns(0, small * 128)]
     if small < big:
@@ -504,21 +506,35 @@
 
     k1_at = pl.multiple_of(jnp.where(upper, depth - k1, 0), 256)
     k2_at = pl.multiple_of(jnp.where(upper, late, k1), 256)
-    early_at = pl.multiple_of(jnp.where(upper, late, 0), 256)
     late_at = pl.multiple_of(jnp.where(upper, 0, depth - late), 256)
-
-    def squares(at, count, c, w):
-        w32 = buf[pl.ds(at, count), pl.ds(c, w)].astype(jnp.float32)
-        return jnp.sum((w32 * w32).reshape(count // 8, 8, w), 0)
-
-    def begin(slot, count, at, deep, add=False):
-        rows = docs[pl.ds(slot, count), :, pl.ds(at, deep)].reshape(count * rows_dev, deep)
-        prod = jnp.dot(rows, buf[pl.ds(at, deep), :], preferred_element_type=jnp.float32)
-        prod = prod.reshape(count, rows_dev, wide)
-        if add:
-            acc[pl.ds(slot, count)] += prod
+    starts = (k1_at, k2_at, late_at)
+
+    def squares(i, c, w):
+        w32 = buf[pl.ds(starts[i], 256), pl.ds(c, w)].astype(jnp.float32)
+        return jnp.sum((w32 * w32).reshape(32, 8, w), 0)
+
+    def turn(i, c, w):
+        turned[i, pl.ds(c, w), :] = buf[pl.ds(starts[i], 256), pl.ds(c, w)].T
+
+    def gather(i):
+        for c, w in chunks:
+            turn(i, c, w)
+        csq[...] = squares(i, 0, wide) + (csq[...] if i else 0.0)
+
+    def times(i, c, w, slot, count):
+        rows = docs[pl.ds(slot, count), :, pl.ds(starts[i], 256)].reshape(count * rows_dev, 256)
+        return lax.dot_general(turned[i, pl.ds(c, w), :], rows, (((1,), (1,)), ((), ())),
+                               preferred_element_type=jnp.float32)
+
+    def begin(slot, count, *phases):
+        where_docs = pl.ds(slot * rows_dev, count * rows_dev)
+        prod = times(phases[0], 0, wide, slot, count)
+        for i in phases[1:]:
+            prod = prod + times(i, 0, wide, slot, count)
+        if phases[0]:
+            acc[:, where_docs] += prod
         else:
-            acc[pl.ds(slot, count)] = prod
+            acc[:, where_docs] = prod
 
     spread(1)
     prepare_ids(0)
@@ -527,8 +543,7 @@
     spread(3)
     relay(1)
     have_docs(2, 0)
-    send_docs(2, 0, 6, 4)
-    share(2, 0)
+    send_docs(2, 6, 4, 0)
     have_ids(4)
     send_ids(4, 6, 2)
     send_ids(4, 5, 1)
@@ -536,126 +551,128 @@
     send_ids(2, 3, 1)
     relay(2)
     have_docs(4, 1)
-    send_docs(4, 1, 6, 2)
-    share(4, 1)
-    have_docs(2, 1)
-    share(2, 1)
+    send_docs(4, 6, 2, 1)
+    have_docs(2, 1, 2)
+    share(2, 0, 1, 2)
     relay(3)
     relay_far(0)
     have_docs(4, 2)
-    send_docs(4, 2, 6, 2)
-    share(4, 2)
-    have_docs(2, 2)
-    share(2, 2)
+    send_docs(4, 6, 2, 2)
     have_ids(6)
     send_ids(6, 7, 1)
     have_docs(1, 0, 1, 2)
-    begin(0, 2, k1_at, k1)
+    gather(0)
+    begin(0, 2, 0)
     relay_far(1)
+    have_ids(1)
     for slot in (1, 2, 3, 4, 5, 6, 7):
-        if slot in (1, 3, 5, 7):
-            have_ids(slot)
         prepare_ids(slot)
     have_docs(4, 0)
-    share(4, 0)
+    share(4, 0, 1, 2)
     relay_far(2)
     have_docs(3, 0, 1, 2)
-    begin(2, 2, k1_at, k1)
-    csq[...] = squares(k1_at, k1, 0, wide)
+    begin(2, 2, 0)
     relay_far(3)
-    begin(0, 2, k2_at, k2, True)
-    begin(2, 2, k2_at, k2, True)
-    csq[...] += squares(k2_at, k2, 0, wide)
-    have_docs(5, 1, 2, 0)
-    begin(4, 2, early_at, k1 + k2)
+    gather(1)
+    begin(0, 2, 1)
+    begin(2, 2, 1)
+    have_docs(5, 0, 1, 2)
+    begin(4, 2, 0, 1)
     for p in (1, 2, 0):
         have_docs(6, p)
-        share(6, p)
-    begin(6, 1, early_at, k1 + k2)
+    share(6, 0, 1, 2)
+    begin(6, 1, 0, 1)
 
     def scales(k):
         c, w = chunks[k]
-        total = jnp.sum(csq[:, pl.ds(c, w)] + squares(late_at, late, c, w), 0, keepdims=True)
-        scale[:, pl.ds(c, w)] = lax.rsqrt(total + epsilon)
-
-    def stage(k, slot):
+        total = jnp.sum(csq[:, pl.ds(c, w)] + squares(2, c, w), 0, keepdims=True)
+        scale[pl.ds(c, w), :] = jnp.broadcast_to(lax.rsqrt(total + epsilon), (128, w)).T
+
+    def stage(k, slot, count):
         c0, w = chunks[k]
-        rows = docs[pl.ds(slot, 2), :, pl.ds(late_at, late)].reshape(2 * rows_dev, late)
-        prod = jnp.dot(rows, buf[pl.ds(late_at, late), pl.ds(c0, w)], preferred_element_type=jnp.float32)
-        for half in (0, 1):
-            for r in range(0, rows_dev, ROWS):
-                rs = pl.ds(r, ROWS)
-                at = half * rows_dev + r
-                if k:
-                    top, hit = mx[slot + half, rs, :], ch[slot + half, rs, :]
-                else:
-                    top = jnp.full((ROWS, 128), -3.0e38, jnp.float32)
-                    hit = jnp.zeros((ROWS, 128), jnp.float32)
-                where_id = idb[slot + half, rs, :]
-                for c in range(0, w, 128):
-                    cols = pl.ds(c0 + c, 128)
-                    v = (acc[slot + half, rs, cols] + prod[at:at + ROWS, c:c + 128]) * scale[:, cols]
-                    hit = jnp.where(where_id == c0 + c, v, hit)
-                    if c0 + c + 128 > small * 128 or (c0 + c + 128 == small * 128 and small == big):
-                        v = jnp.where(lane < reach - (c0 + c), v, -3.0e38)
-                    top = jnp.maximum(top, v)
-                mx[slot + half, rs, :] = top
-                ch[slot + half, rs, :] = hit
+        prod = times(2, c0, w, slot, count)
+        for d in range(0, count * rows_dev, 128):
+            at = pl.ds(slot * rows_dev + d, 128)
+            if k:
+                top, hit = mx[:, at], ch[:, at]
+            else:
+                top = jnp.full((GROUP, 128), -3.0e38, jnp.float32)
+                hit = jnp.zeros((GROUP, 128), jnp.float32)
+            where_id = idb[:, at]
+            for c in range(0, w, GROUP):
+                rows = pl.ds(c0 + c, GROUP)
+                v = (acc[rows, at] + prod[c:c + GROUP, d:d + 128]) * scale[rows, :]
+                hit = jnp.where(where_id == c0 + c, v, hit)
+                if c0 + c + 128 > small * 128:
+                    v = jnp.where(down < reach - (c0 + c), v, -3.0e38)
+                top = jnp.maximum(top, v)
+            mx[:, at] = top
+            ch[:, at] = hit
 
     def reduced(slot):
-        return (jnp.max(mx[slot].T, 0, keepdims=True), jnp.sum(ch[slot].T, 0, keepdims=True))
+        at = pl.ds(slot * rows_dev, rows_dev)
+        return jnp.max(mx[:, at], 0, keepdims=True), jnp.sum(ch[:, at], 0, keepdims=True)
 
     def give(slot):
         best, chosen = reduced(slot)
         res[slot, 0:1, :] = best
         res[slot, 1:2, :] = chosen
-        start(lambda: remote(res.at[slot], got.at[slot], r_send.at[slot], r_recv.at[slot], device(slot)))
-
-    landed(z - 3 * out, 0, end)
-    landed(z - 3 * out, 1, end)
-    final = len(chunks) - 1
-    for k in range(final):
-        last_landed(k)
-        scales(k)
-        for slot in (0, 2, 4):
-            stage(k, slot)
-        if k == 0:
-            have_docs(7, 1, 2, 0)
-            begin(7, 1, early_at, k1 + k2)
-        stage(k, 6)
-    last_landed(final)
-    scales(final)
-    stage(final, 6)
-    stage(final, 2)
-    give(7)
-    give(6)
-    stage(final, 4)
-    give(3)
-    give(2)
-    stage(final, 0)
-    give(5)
-    give(4)
-    give(1)
-    best, chosen = reduced(0)
+        remote(res.at[slot], got.at[slot], result_sent, r_recv, device(slot)).start()
+
     x32 = docs[0].astype(jnp.float32)
     sq = x32 * x32
     total = sq[:, 0:128]
     for c in range(128, depth, 128):
         total = total + sq[:, c:c + 128]
     scale_x = lax.rsqrt(jnp.sum(total.T, 0, keepdims=True) + epsilon)
-    for slot in (1, 4, 5, 2, 3, 6, 7):
-        remote(res.at[slot], got.at[slot], r_send.at[slot], r_recv.at[slot], device(slot)).wait_recv()
+
+    landed(z - 3 * out, 0, end)
+    landed(z - 3 * out, 1, end)
+    final = len(chunks) - 1
+    for k in range(final):
+        last_landed(k)
+        turn(2, *chunks[k])
+        scales(k)
+        for slot in (0, 2, 4):
+            stage(k, slot, 2)
+        if k == 0:
+            have_docs(7, 0, 1, 2)
+            begin(7, 1, 0, 1)
+        stage(k, 6, 2)
+    last_landed(final)
+    turn(2, *chunks[final])
+    scales(final)
+    stage(final, 6, 2)
+    stage(final, 2, 2)
+    give(7)
+    give(6)
+    stage(final, 4, 2)
+    give(3)
+    give(2)
+    stage(final, 0, 2)
+    give(5)
+    give(4)
+    give(1)
+    best, chosen = reduced(0)
+    everyone = pl.ds(1, 7)
+    remote(got.at[everyone], got.at[everyone], result_sent, r_recv, device(1)).wait_recv()
+    for slot in range(1, 8):
         best = jnp.maximum(best, got[slot, 0:1, :])
         chosen = chosen + got[slot, 1:2, :]
     near_out[...] = best * scale_x
     chosen_out[...] = chosen * scale_x
-    for entry in pending:
-        if len(entry) == 2:
-            cond, make = entry
-            when(cond, lambda: make().wait_send())
-        else:
-            c, cond, make = entry
-            sized(c, cond, lambda w: make(w).wait_send())
+
+    def sent(ref, sem):
+        remote(ref, ref, sem, r_recv, device(1)).wait_send()
+
+    sent(res.at[everyone], result_sent)
+    sent(docs.at[everyone], doc_sent)
+    sent(ids.at[everyone], id_sent)
+    layer = 4 * feat
+    sized(core, inner, lambda w: sent(buf.at[pl.ds(0, 3 * layer), pl.ds(0, w)], outward))
+    sized(core, inner, lambda w: sent(buf.at[pl.ds(0, 2 * layer), pl.ds(0, w)], inward))
+    sized(core, end, lambda w: sent(buf.at[pl.ds(0, layer), pl.ds(0, w)], inward))
+    sized(core, None, lambda w: sent(own.at[:, pl.ds(0, 2 * per * 128 - w)], traded))
 
 
 def by_layers(docs, centroids, assigned):
@@ -679,17 +696,16 @@
             pltpu.VMEM((depth, wide), jnp.bfloat16),
             pltpu.VMEM((8, rows_dev, depth), jnp.bfloat16),
             pltpu.VMEM((8, 1, rows_dev), jnp.int32),
-            pltpu.VMEM((8, rows_dev, wide), jnp.float32),
-            pltpu.VMEM((8, rows_dev, 128), jnp.int32),
-            pltpu.VMEM((8, rows_dev, 128), jnp.float32),
-            pltpu.VMEM((8, rows_dev, 128), jnp.float32),
+            pltpu.VMEM((3, wide, 256), jnp.bfloat16),
+            pltpu.VMEM((wide, 8 * rows_dev), jnp.float32),
+            pltpu.VMEM((GROUP, 8 * rows_dev), jnp.int32),
+            pltpu.VMEM((GROUP, 8 * rows_dev), jnp.float32),
+            pltpu.VMEM((GROUP, 8 * rows_dev), jnp.float32),
             pltpu.VMEM((8, wide), jnp.float32),
-            pltpu.VMEM((1, wide), jnp.float32),
+            pltpu.VMEM((wide, 128), jnp.float32),
             pltpu.VMEM((8, 2, rows_dev), jnp.float32),
             pltpu.VMEM((8, 2, rows_dev), jnp.float32),
-            dma((4,)),
-            dma((4,)), dma((nz, 4)), dma((2, 3, 4)), dma((-(-wide // 256),)), dma((-(-wide // 256),)),
-            dma((8, 3)), dma((8, 3)), dma((8,)), dma((8,)), dma((8,)), dma((8,)),
+            dma((4,)), dma((6,)), dma((nz, 4)), dma((-(-wide // 256),)), dma((12,)), dma((4,)), dma,
         ],
         compiler_params=pltpu.CompilerParams(collective_id=0, has_side_effects=True),
         name="layer_distances",
@@ -702,7 +718,7 @@
     n_clu, feat = lax.axis_size("clu"), centroids.shape[1]
     return (lax.axis_size("doc") == 2 and n_clu == 16 and tiles % 2 == 0 and tiles >= 4
             and feat % 16 == 0 and docs.shape[0] % 128 == 0 and docs.shape[1] % 256 == 0
-            and docs.shape[1] == n_clu * feat and 8 * feat >= 256)
+            and docs.shape[1] == n_clu * feat == 3 * 256)
 
 
 def on_device(docs, centroids, assigned):

time: 30.4 us -> 29.8 us (0.980)
  Pallas kernels: 29 us -> 28.5 us
    pallas_call x1, Pallas kernels: 29 us -> 28.5 us  [by_layers(): pl.pallas_call(functools.partial(layer_kernel, nz, feat), out_shape=(line...]
where the time goes in v3:
time: 29.8 us; the launch traced here: 29.7 us
  Pallas kernels  28.5 us (96%)
  between operations  0.64 us (2%)
  other arithmetic  0.57 us (2%)
    pallas_call x1, Pallas kernels, by_layers(): pl.pallas_call(functools.partial(layer_kernel, nz, feat), out_shape=(line...  28.5 us

profile of v3, /device:TPU:0, one launch (start us, length us, event | category | flops | bytes accessed | tf_op | source)
XLA Modules:
  0.0 29.7 jit_solution(3972158454704734611)
XLA Ops:
  0.6 28.5 %layer_distances.1 = (f32[1,256]{1,0:T(1,128)S(1)}, f32[1,256]{1,0:T(1,128)S(1)}) custom-call(bf16[256,768]{1,0:T(8,128)(2,1)} %docs_in.1, bf16[48,2752]{1,0:T(8,128)(2,1)} %bitcast.4, s32[1,256]{1,0:T(1,128)} %bitcast.5), custom_call_target="tpu_custom_call" | custom-call | tf_op jit(solution)/shard_map/layer_distances/pallas_call | solution.py:688
  29.1 0.6 %broadcast_subtract_fusion = (f32[1,256]{1,0:T(1,128)}, f32[1,256]{1,0:T(1,128)}) fusion(f32[1,256]{1,0:T(1,128)S(1)} %get-tuple-element.5, f32[1,256]{1,0:T(1,128)S(1)} %get-tuple-element.4), kind=kLoop, calls=%fused_computation | loop fusion | flops 512 | bytes 4096 | tf_op jit(solution)/shard_map/sub | solution.py:713

commit v4 on v3

--- a/solution.py
+++ b/solution.py
@@ -10,7 +10,7 @@
 epsilon = 1e-06
 PIECES = 4
 ROWS = 64
-GROUP = 32
+GROUP = 16
 MESH = pl.DeviceIdType.MESH
 
 
@@ -292,7 +292,7 @@
 
 
 def layer_kernel(nz, feat, docs_in, cents_in, ids_in, near_out, chosen_out,
-                 own, raw, buf, docs, ids, turned, acc, idb, mx, ch, csq, scale, res, got,
+                 own, raw, buf, docs, flat, ids, turned, acc, idb, mx, ch, csq, scale, res, got,
                  local_sem, send_sem, c_recv, last_recv, d_recv, i_recv, r_recv):
     width = cents_in.shape[1]
     rows_dev, depth = docs_in.shape
@@ -521,10 +521,14 @@
             turn(i, c, w)
         csq[...] = squares(i, 0, wide) + (csq[...] if i else 0.0)
 
+    def flatten(*slots):
+        for slot in slots:
+            flat[:, pl.ds(slot * rows_dev, rows_dev)] = docs[slot].T
+
     def times(i, c, w, slot, count):
-        rows = docs[pl.ds(slot, count), :, pl.ds(starts[i], 256)].reshape(count * rows_dev, 256)
-        return lax.dot_general(turned[i, pl.ds(c, w), :], rows, (((1,), (1,)), ((), ())),
-                               preferred_element_type=jnp.float32)
+        return jnp.dot(turned[i, pl.ds(c, w), :],
+                       flat[pl.ds(starts[i], 256), pl.ds(slot * rows_dev, count * rows_dev)],
+                       preferred_element_type=jnp.float32)
 
     def begin(slot, count, *phases):
         where_docs = pl.ds(slot * rows_dev, count * rows_dev)
@@ -538,6 +542,7 @@
 
     spread(1)
     prepare_ids(0)
+    flatten(0)
     spread(2)
     relay(0)
     spread(3)
@@ -552,62 +557,65 @@
     relay(2)
     have_docs(4, 1)
     send_docs(4, 6, 2, 1)
+    have_docs(1, 0, 1, 2)
+    flatten(1)
+    relay(3)
+    relay_far(0)
     have_docs(2, 1, 2)
     share(2, 0, 1, 2)
-    relay(3)
-    relay_far(0)
     have_docs(4, 2)
     send_docs(4, 6, 2, 2)
     have_ids(6)
     send_ids(6, 7, 1)
-    have_docs(1, 0, 1, 2)
+    relay_far(1)
     gather(0)
     begin(0, 2, 0)
-    relay_far(1)
+    flatten(2)
     have_ids(1)
     for slot in (1, 2, 3, 4, 5, 6, 7):
         prepare_ids(slot)
+    relay_far(2)
     have_docs(4, 0)
     share(4, 0, 1, 2)
-    relay_far(2)
     have_docs(3, 0, 1, 2)
+    flatten(3)
     begin(2, 2, 0)
     relay_far(3)
     gather(1)
+    flatten(4)
     begin(0, 2, 1)
     begin(2, 2, 1)
     have_docs(5, 0, 1, 2)
+    flatten(5)
     begin(4, 2, 0, 1)
     for p in (1, 2, 0):
         have_docs(6, p)
     share(6, 0, 1, 2)
-    begin(6, 1, 0, 1)
-
-    def scales(k):
-        c, w = chunks[k]
+    flatten(6)
+
+    def scales(c, w):
         total = jnp.sum(csq[:, pl.ds(c, w)] + squares(2, c, w), 0, keepdims=True)
         scale[pl.ds(c, w), :] = jnp.broadcast_to(lax.rsqrt(total + epsilon), (128, w)).T
 
-    def stage(k, slot, count):
-        c0, w = chunks[k]
+    def stage(c0, w, slot, count):
         prod = times(2, c0, w, slot, count)
-        for d in range(0, count * rows_dev, 128):
-            at = pl.ds(slot * rows_dev + d, 128)
-            if k:
-                top, hit = mx[:, at], ch[:, at]
-            else:
-                top = jnp.full((GROUP, 128), -3.0e38, jnp.float32)
-                hit = jnp.zeros((GROUP, 128), jnp.float32)
-            where_id = idb[:, at]
-            for c in range(0, w, GROUP):
-                rows = pl.ds(c0 + c, GROUP)
-                v = (acc[rows, at] + prod[c:c + GROUP, d:d + 128]) * scale[rows, :]
-                hit = jnp.where(where_id == c0 + c, v, hit)
+        spots = [pl.ds(slot * rows_dev + d, 128) for d in range(0, count * rows_dev, 128)]
+        if c0:
+            tops, hits = [mx[:, at] for at in spots], [ch[:, at] for at in spots]
+        else:
+            tops = [jnp.full((GROUP, 128), -3.0e38, jnp.float32)] * len(spots)
+            hits = [jnp.zeros((GROUP, 128), jnp.float32)] * len(spots)
+        for c in range(0, w, GROUP):
+            rows = pl.ds(c0 + c, GROUP)
+            by = scale[rows, :]
+            for n, at in enumerate(spots):
+                v = (acc[rows, at] + prod[c:c + GROUP, n * 128:n * 128 + 128]) * by
+                hits[n] = jnp.where(idb[:, at] == c0 + c, v, hits[n])
                 if c0 + c + 128 > small * 128:
                     v = jnp.where(down < reach - (c0 + c), v, -3.0e38)
-                top = jnp.maximum(top, v)
-            mx[:, at] = top
-            ch[:, at] = hit
+                tops[n] = jnp.maximum(tops[n], v)
+        for n, at in enumerate(spots):
+            mx[:, at], ch[:, at] = tops[n], hits[n]
 
     def reduced(slot):
         at = pl.ds(slot * rows_dev, rows_dev)
@@ -629,30 +637,38 @@
     landed(z - 3 * out, 0, end)
     landed(z - 3 * out, 1, end)
     final = len(chunks) - 1
-    for k in range(final):
-        last_landed(k)
-        turn(2, *chunks[k])
-        scales(k)
+    for i in range(final):
+        last_landed(i)
+        c, w = chunks[i]
+        turn(2, c, w)
+        scales(c, w)
         for slot in (0, 2, 4):
-            stage(k, slot, 2)
-        if k == 0:
+            stage(c, w, slot, 2)
+        if i == 0:
             have_docs(7, 0, 1, 2)
-            begin(7, 1, 0, 1)
-        stage(k, 6, 2)
+            flatten(7)
+            begin(6, 2, 0, 1)
+        stage(c, w, 6, 2)
     last_landed(final)
-    turn(2, *chunks[final])
-    scales(final)
-    stage(final, 6, 2)
-    stage(final, 2, 2)
-    give(7)
-    give(6)
-    stage(final, 4, 2)
-    give(3)
-    give(2)
-    stage(final, 0, 2)
-    give(5)
-    give(4)
-    give(1)
+
+    def finish(have):
+        c = chunks[final][0]
+        w = have - c
+        turn(2, c, w)
+        scales(c, w)
+        stage(c, w, 6, 2)
+        stage(c, w, 2, 2)
+        give(7)
+        give(6)
+        stage(c, w, 4, 2)
+        give(3)
+        give(2)
+        stage(c, w, 0, 2)
+        give(5)
+        give(4)
+        give(1)
+
+    sized(core, None, finish)
     best, chosen = reduced(0)
     everyone = pl.ds(1, 7)
     remote(got.at[everyone], got.at[everyone], result_sent, r_recv, device(1)).wait_recv()
@@ -695,6 +711,7 @@
             pltpu.VMEM((feat, width % 128 or 128), jnp.bfloat16),
             pltpu.VMEM((depth, wide), jnp.bfloat16),
             pltpu.VMEM((8, rows_dev, depth), jnp.bfloat16),
+            pltpu.VMEM((depth, 8 * rows_dev), jnp.bfloat16),
             pltpu.VMEM((8, 1, rows_dev), jnp.int32),
             pltpu.VMEM((3, wide, 256), jnp.bfloat16),
             pltpu.VMEM((wide, 8 * rows_dev), jnp.float32),

time: 29.8 us -> 29.2 us (0.980)
  Pallas kernels: 28.5 us -> 27.8 us
    pallas_call x1, Pallas kernels: 28.5 us -> 27.8 us  [by_layers(): pl.pallas_call(functools.partial(layer_kernel, nz, feat), out_shape=(line...]
where the time goes in v4:
time: 29.2 us; the launch traced here: 29 us
  Pallas kernels  27.8 us (95%)
  between operations  0.64 us (2%)
  other arithmetic  0.57 us (2%)
    pallas_call x1, Pallas kernels, by_layers(): pl.pallas_call(functools.partial(layer_kernel, nz, feat), out_shape=(line...  27.8 us

profile of v4, /device:TPU:0, one launch (start us, length us, event | category | flops | bytes accessed | tf_op | source)
XLA Modules:
  0.0 29.0 jit_solution(6805966644766287981)
XLA Ops:
  0.6 27.8 %layer_distances.1 = (f32[1,256]{1,0:T(1,128)S(1)}, f32[1,256]{1,0:T(1,128)S(1)}) custom-call(bf16[256,768]{1,0:T(8,128)(2,1)} %docs_in.1, bf16[48,2752]{1,0:T(8,128)(2,1)} %bitcast.4, s32[1,256]{1,0:T(1,128)} %bitcast.5), custom_call_target="tpu_custom_call" | custom-call | tf_op jit(solution)/shard_map/layer_distances/pallas_call | solution.py:704
  28.5 0.6 %broadcast_subtract_fusion = (f32[1,256]{1,0:T(1,128)}, f32[1,256]{1,0:T(1,128)}) fusion(f32[1,256]{1,0:T(1,128)S(1)} %get-tuple-element.5, f32[1,256]{1,0:T(1,128)S(1)} %get-tuple-element.4), kind=kLoop, calls=%fused_computation | loop fusion | flops 512 | bytes 4096 | tf_op jit(solution)/shard_map/sub | solution.py:730

commit v5 on v4

--- a/solution.py
+++ b/solution.py
@@ -636,19 +636,17 @@
 
     landed(z - 3 * out, 0, end)
     landed(z - 3 * out, 1, end)
+    have_docs(7, 0, 1, 2)
+    flatten(7)
+    begin(6, 2, 0, 1)
     final = len(chunks) - 1
     for i in range(final):
         last_landed(i)
         c, w = chunks[i]
         turn(2, c, w)
         scales(c, w)
-        for slot in (0, 2, 4):
+        for slot in (0, 2, 4, 6):
             stage(c, w, slot, 2)
-        if i == 0:
-            have_docs(7, 0, 1, 2)
-            flatten(7)
-            begin(6, 2, 0, 1)
-        stage(c, w, 6, 2)
     last_landed(final)
 
     def finish(have):
@@ -657,15 +655,15 @@
         turn(2, c, w)
         scales(c, w)
         stage(c, w, 6, 2)
+        give(6)
+        give(7)
         stage(c, w, 2, 2)
-        give(7)
-        give(6)
+        give(2)
+        give(3)
         stage(c, w, 4, 2)
-        give(3)
-        give(2)
+        give(4)
+        give(5)
         stage(c, w, 0, 2)
-        give(5)
-        give(4)
         give(1)
 
     sized(core, None, finish)

time: 29.2 us -> 29 us (level)
  no operation moved by 1% of the time
where the time goes in v5:
time: 29 us; the launch traced here: 28.9 us
  Pallas kernels  27.7 us (96%)
  between operations  0.64 us (2%)
  other arithmetic  0.57 us (2%)
    pallas_call x1, Pallas kernels, by_layers(): pl.pallas_call(functools.partial(layer_kernel, nz, feat), out_shape=(line...  27.7 us

profile of v5, /device:TPU:0, one launch (start us, length us, event | category | flops | bytes accessed | tf_op | source)
XLA Modules:
  0.0 28.9 jit_solution(9693515009117138586)
XLA Ops:
  0.6 27.7 %layer_distances.1 = (f32[1,256]{1,0:T(1,128)S(1)}, f32[1,256]{1,0:T(1,128)S(1)}) custom-call(bf16[256,768]{1,0:T(8,128)(2,1)} %docs_in.1, bf16[48,2752]{1,0:T(8,128)(2,1)} %bitcast.4, s32[1,256]{1,0:T(1,128)} %bitcast.5), custom_call_target="tpu_custom_call" | custom-call | tf_op jit(solution)/shard_map/layer_distances/pallas_call | solution.py:702
  28.3 0.6 %broadcast_subtract_fusion = (f32[1,256]{1,0:T(1,128)}, f32[1,256]{1,0:T(1,128)}) fusion(f32[1,256]{1,0:T(1,128)S(1)} %get-tuple-element.5, f32[1,256]{1,0:T(1,128)S(1)} %get-tuple-element.4), kind=kLoop, calls=%fused_computation | loop fusion | flops 512 | bytes 4096 | tf_op jit(solution)/shard_map/sub | solution.py:728

commit v6 on v5

--- a/solution.py
+++ b/solution.py
@@ -308,7 +308,7 @@
     a = rows_dev * 5 // 16 // 16 * 16
     b = (rows_dev - a) // 32 * 16
     spans = ((0, a), (a, b), (a + b, rows_dev - a - b))
-    chunks = tuple((c, min(256, wide - c)) for c in range(0, wide, 256))
+    cuts = {w: (0, 256, (w - 1) // 256 * 256, w) for w in (small * 128, wide)}
 
     clu, doc = lax.axis_index("clu"), lax.axis_index("doc")
     core, chip = lax.rem(clu, 2), lax.div(clu, 2)
@@ -428,15 +428,14 @@
 
     def pair(layer, k, w):
         rows = pl.ds(pl.multiple_of((layer * 2 + 1 - x) * 2 * feat, 16), 2 * feat)
-        c = chunks[k][0]
-        return buf.at[rows, pl.ds(c, min(w, c + chunks[k][1]) - c)]
+        return buf.at[rows, pl.ds(cuts[w][k], cuts[w][k + 1] - cuts[w][k])]
 
     def relay_far(j):
         landed(z - 2 * out, j)
         if j < 2:
             carry(z - 2 * out, j, 0, 2, inner)
         elif j == 3:
-            for k in range(len(chunks)):
+            for k in range(3):
                 start_sized(lambda w, k=k: remote(
                     pair(z - 2 * out, k, w), pair(z - 2 * out, k, w), outward, last_recv.at[k],
                     device(0, out)), core, inner)
@@ -517,8 +516,8 @@
         turned[i, pl.ds(c, w), :] = buf[pl.ds(starts[i], 256), pl.ds(c, w)].T
 
     def gather(i):
-        for c, w in chunks:
-            turn(i, c, w)
+        for c in range(0, wide, 256):
+            turn(i, c, min(256, wide - c))
         csq[...] = squares(i, 0, wide) + (csq[...] if i else 0.0)
 
     def flatten(*slots):
@@ -577,10 +576,10 @@
     relay_far(2)
     have_docs(4, 0)
     share(4, 0, 1, 2)
+    relay_far(3)
     have_docs(3, 0, 1, 2)
     flatten(3)
     begin(2, 2, 0)
-    relay_far(3)
     gather(1)
     flatten(4)
     begin(0, 2, 1)
@@ -639,34 +638,21 @@
     have_docs(7, 0, 1, 2)
     flatten(7)
     begin(6, 2, 0, 1)
-    final = len(chunks) - 1
-    for i in range(final):
-        last_landed(i)
-        c, w = chunks[i]
+
+    def advance(k, have):
+        c, w = cuts[have][k], cuts[have][k + 1] - cuts[have][k]
         turn(2, c, w)
         scales(c, w)
-        for slot in (0, 2, 4, 6):
+        for slot in (6, 2, 4, 0):
             stage(c, w, slot, 2)
-    last_landed(final)
-
-    def finish(have):
-        c = chunks[final][0]
-        w = have - c
-        turn(2, c, w)
-        scales(c, w)
-        stage(c, w, 6, 2)
-        give(6)
-        give(7)
-        stage(c, w, 2, 2)
-        give(2)
-        give(3)
-        stage(c, w, 4, 2)
-        give(4)
-        give(5)
-        stage(c, w, 0, 2)
-        give(1)
-
-    sized(core, None, finish)
+            if k == 2:
+                give(slot + 1)
+                if slot:
+                    give(slot)
+
+    for k in range(3):
+        last_landed(k)
+        sized(core, None, functools.partial(advance, k))
     best, chosen = reduced(0)
     everyone = pl.ds(1, 7)
     remote(got.at[everyone], got.at[everyone], result_sent, r_recv, device(1)).wait_recv()
@@ -720,7 +706,7 @@
             pltpu.VMEM((wide, 128), jnp.float32),
             pltpu.VMEM((8, 2, rows_dev), jnp.float32),
             pltpu.VMEM((8, 2, rows_dev), jnp.float32),
-            dma((4,)), dma((6,)), dma((nz, 4)), dma((-(-wide // 256),)), dma((12,)), dma((4,)), dma,
+            dma((4,)), dma((6,)), dma((nz, 4)), dma((3,)), dma((12,)), dma((4,)), dma,
         ],
         compiler_params=pltpu.CompilerParams(collective_id=0, has_side_effects=True),
         name="layer_distances",
@@ -731,7 +717,7 @@
 def fits_layers(docs, centroids):
     tiles = -(-centroids.shape[0] // 128)
     n_clu, feat = lax.axis_size("clu"), centroids.shape[1]
-    return (lax.axis_size("doc") == 2 and n_clu == 16 and tiles % 2 == 0 and tiles >= 4
+    return (lax.axis_size("doc") == 2 and n_clu == 16 and tiles % 2 == 0 and tiles >= 20
             and feat % 16 == 0 and docs.shape[0] % 128 == 0 and docs.shape[1] % 256 == 0
             and docs.shape[1] == n_clu * feat == 3 * 256)
 

time: 29 us -> 29 us (level)
  no operation moved by 1% of the time
where the time goes in v6:
time: 29 us; the launch traced here: 28.8 us
  Pallas kernels  27.6 us (95%)
  between operations  0.64 us (2%)
  other arithmetic  0.57 us (2%)
    pallas_call x1, Pallas kernels, by_layers(): pl.pallas_call(functools.partial(layer_kernel, nz, feat), out_shape=(line...  27.6 us

profile of v6, /device:TPU:0, one launch (start us, length us, event | category | flops | bytes accessed | tf_op | source)
XLA Modules:
  0.0 28.8 jit_solution(248643677949885529)
XLA Ops:
  0.6 27.6 %layer_distances.1 = (f32[1,256]{1,0:T(1,128)S(1)}, f32[1,256]{1,0:T(1,128)S(1)}) custom-call(bf16[256,768]{1,0:T(8,128)(2,1)} %docs_in.1, bf16[48,2752]{1,0:T(8,128)(2,1)} %bitcast.4, s32[1,256]{1,0:T(1,128)} %bitcast.5), custom_call_target="tpu_custom_call" | custom-call | tf_op jit(solution)/shard_map/layer_distances/pallas_call | solution.py:688
  28.3 0.6 %broadcast_subtract_fusion = (f32[1,256]{1,0:T(1,128)}, f32[1,256]{1,0:T(1,128)}) fusion(f32[1,256]{1,0:T(1,128)S(1)} %get-tuple-element.5, f32[1,256]{1,0:T(1,128)S(1)} %get-tuple-element.4), kind=kLoop, calls=%fused_computation | loop fusion | flops 512 | bytes 4096 | tf_op jit(solution)/shard_map/sub | solution.py:714

commit v7 on v6

--- a/solution.py
+++ b/solution.py
@@ -434,11 +434,12 @@
         landed(z - 2 * out, j)
         if j < 2:
             carry(z - 2 * out, j, 0, 2, inner)
-        elif j == 3:
-            for k in range(3):
-                start_sized(lambda w, k=k: remote(
-                    pair(z - 2 * out, k, w), pair(z - 2 * out, k, w), outward, last_recv.at[k],
-                    device(0, out)), core, inner)
+
+    def send_last(cond):
+        for k in range(3):
+            start_sized(lambda w, k=k: remote(
+                pair(z - 2 * out, k, w), pair(z - 2 * out, k, w), outward, last_recv.at[k],
+                device(0, out)), core, inner & cond)
 
     def last_landed(k):
         sized(core, end, lambda w: remote(
@@ -531,13 +532,17 @@
 
     def begin(slot, count, *phases):
         where_docs = pl.ds(slot * rows_dev, count * rows_dev)
-        prod = times(phases[0], 0, wide, slot, count)
-        for i in phases[1:]:
-            prod = prod + times(i, 0, wide, slot, count)
-        if phases[0]:
-            acc[:, where_docs] += prod
-        else:
-            acc[:, where_docs] = prod
+
+        def add(w):
+            prod = times(phases[0], 0, w, slot, count)
+            for i in phases[1:]:
+                prod = prod + times(i, 0, w, slot, count)
+            if phases[0]:
+                acc[pl.ds(0, w), where_docs] += prod
+            else:
+                acc[pl.ds(0, w), where_docs] = prod
+
+        sized(core, None, add)
 
     spread(1)
     prepare_ids(0)
@@ -577,19 +582,26 @@
     have_docs(4, 0)
     share(4, 0, 1, 2)
     relay_far(3)
+    send_last(core == 0)
     have_docs(3, 0, 1, 2)
     flatten(3)
     begin(2, 2, 0)
     gather(1)
+    send_last(core == 1)
     flatten(4)
     begin(0, 2, 1)
     begin(2, 2, 1)
+
+    def share_far():
+        for p in (1, 2, 0):
+            have_docs(6, p)
+        share(6, 0, 1, 2)
+
+    pl.when(core == 1)(share_far)
     have_docs(5, 0, 1, 2)
     flatten(5)
+    pl.when(core == 0)(share_far)
     begin(4, 2, 0, 1)
-    for p in (1, 2, 0):
-        have_docs(6, p)
-    share(6, 0, 1, 2)
     flatten(6)
 
     def scales(c, w):

time: 29 us -> 28.9 us (level)
  no operation moved by 1% of the time
where the time goes in v7:
time: 28.9 us; the launch traced here: 28.7 us
  Pallas kernels  27.5 us (95%)
  between operations  0.64 us (2%)
  other arithmetic  0.57 us (2%)
    pallas_call x1, Pallas kernels, by_layers(): pl.pallas_call(functools.partial(layer_kernel, nz, feat), out_shape=(line...  27.5 us

profile of v7, /device:TPU:0, one launch (start us, length us, event | category | flops | bytes accessed | tf_op | source)
XLA Modules:
  0.0 28.7 jit_solution(4031630341087586837)
XLA Ops:
  0.6 27.5 %layer_distances.1 = (f32[1,256]{1,0:T(1,128)S(1)}, f32[1,256]{1,0:T(1,128)S(1)}) custom-call(bf16[256,768]{1,0:T(8,128)(2,1)} %docs_in.1, bf16[48,2752]{1,0:T(8,128)(2,1)} %bitcast.4, s32[1,256]{1,0:T(1,128)} %bitcast.5), custom_call_target="tpu_custom_call" | custom-call | tf_op jit(solution)/shard_map/layer_distances/pallas_call | solution.py:700
  28.2 0.6 %broadcast_subtract_fusion = (f32[1,256]{1,0:T(1,128)}, f32[1,256]{1,0:T(1,128)}) fusion(f32[1,256]{1,0:T(1,128)S(1)} %get-tuple-element.5, f32[1,256]{1,0:T(1,128)S(1)} %get-tuple-element.4), kind=kLoop, calls=%fused_computation | loop fusion | flops 512 | bytes 4096 | tf_op jit(solution)/shard_map/sub | solution.py:726

commit v8 on v7

--- a/solution.py
+++ b/solution.py
@@ -292,23 +292,24 @@
 
 
 def layer_kernel(nz, feat, docs_in, cents_in, ids_in, near_out, chosen_out,
-                 own, raw, buf, docs, flat, ids, turned, acc, idb, mx, ch, csq, scale, res, got,
+                 own, raw, ends, buf, docs, flat, ids, turned, acc, idb, mx, ch, csq, scale, res, got,
                  local_sem, send_sem, c_recv, last_recv, d_recv, i_recv, r_recv):
     width = cents_in.shape[1]
     rows_dev, depth = docs_in.shape
-    tiles = own.shape[1] // 128
-    per = tiles // 2
-    small = per // 2
-    big = per - small
-    wide = big * 128
+    half = width // 2
+    count, extra = half // 128, half % 128
+    small = count // 2 * 128
+    wide = small + extra
+    turn_at = (count + 1) * 128
     full = width // 128 * 128
+    rest = width - full
     late = -(-4 * feat // 256) * 256
     k1 = 8 * feat // 256 * 256
     k2 = depth - late - k1
     a = rows_dev * 5 // 16 // 16 * 16
     b = (rows_dev - a) // 32 * 16
     spans = ((0, a), (a, b), (a + b, rows_dev - a - b))
-    cuts = {w: (0, 256, (w - 1) // 256 * 256, w) for w in (small * 128, wide)}
+    cuts = {w: (0, 256, (w - 1) // 256 * 256, w) for w in (small, wide)}
 
     clu, doc = lax.axis_index("clu"), lax.axis_index("doc")
     core, chip = lax.rem(clu, 2), lax.div(clu, 2)
@@ -332,19 +333,20 @@
     def both(p, q):
         return q if p is None else p if q is None else p & q
 
-    sizes = ((None, big),) if big == small else ((1, big), (0, small))
-
     def sized(c, cond, body):
-        for value, count in sizes:
-            when(both(cond, None if value is None else c == value), functools.partial(body, count * 128))
+        for value, w in ((1, wide), (0, small)):
+            when(both(cond, c == value), functools.partial(body, w))
 
     own_copy = pltpu.make_async_copy(cents_in.at[:, pl.ds(0, full)], own.at[:, pl.ds(0, full)], local_sem.at[0])
     docs_copy = pltpu.make_async_copy(docs_in, docs.at[0], local_sem.at[1])
     ids_copy = pltpu.make_async_copy(ids_in, ids.at[0], local_sem.at[2])
     own_copy.start()
-    if full < width:
-        raw_copy = pltpu.make_async_copy(cents_in.at[:, pl.ds(full, width - full)], raw, local_sem.at[3])
-        raw_copy.start()
+    raw_copy = pltpu.make_async_copy(cents_in.at[:, pl.ds(full, rest)], raw, local_sem.at[3])
+    raw_copy.start()
+    end_copies = [pltpu.make_async_copy(cents_in.at[:, pl.ds(k * turn_at + small, small)],
+                                        ends.at[k, :, pl.ds(0, small)], local_sem.at[4 + k]) for k in (0, 1)]
+    for copy in end_copies:
+        copy.start()
     docs_copy.start()
     ids_copy.start()
 
@@ -357,20 +359,23 @@
     greet(device(0, -out))
     for r in (4, 5, 2, 1):
         greet(device(r))
-    if small < big:
-        @pl.when(core == 0)
-        def _():
-            buf[:, pl.ds(small * 128, 128)] = jnp.zeros((buf.shape[0], 128), buf.dtype)
-    if full < width:
-        raw_copy.wait()
-        own[:, pl.ds(full, 128)] = jnp.concatenate(
-            [raw[...], jnp.zeros((feat, full + 128 - width), raw.dtype)], axis=1)
+
+    @pl.when(core == 0)
+    def _():
+        buf[:, pl.ds(small, extra)] = jnp.zeros((buf.shape[0], extra), buf.dtype)
+
     own_copy.wait()
+    raw_copy.wait()
+    middle = own[:, pl.ds(turn_at - 128, 128)]
+    ends[0, :, pl.ds(small, extra)] = middle[:, 0:extra]
+    ends[1, :, pl.ds(small, extra)] = jnp.concatenate([raw[...], middle[:, extra:128]], axis=1)
+    for copy in end_copies:
+        copy.wait()
     docs_copy.wait()
     ids_copy.wait()
     pl.semaphore_wait(barrier, 5 + inner.astype(jnp.int32))
 
-    outward, inward, traded, doc_sent, id_sent, result_sent = (send_sem.at[i] for i in range(6))
+    outward, inward, doc_sent, id_sent, result_sent, traded, traded_wide = (send_sem.at[i] for i in range(7))
 
     def start(make, cond=None):
         when(cond, lambda: make().start())
@@ -389,17 +394,18 @@
         there = (layer * 2 + (1 - x if r // 4 else x)) * 2 + (1 - core if r % 2 else core)
         return pl.ds(pl.multiple_of(there * feat, 16), feat)
 
-    def columns(r, w):
+    def piece(r, w):
         xd = 1 - x if r // 4 else x
-        cd = 1 - core if r % 2 else core
-        return pl.ds(pl.multiple_of((xd * per + cd * small) * 128, 128), w)
+        if w == wide:
+            return ends.at[xd]
+        return own.at[:, pl.ds(pl.multiple_of(xd * turn_at, 128), w)]
 
     mine = source(z, 0)
 
     def exchange(j):
         r = near[j]
-        start_sized(lambda w: remote(own.at[:, columns(r, w)], buf.at[mine, pl.ds(0, w)],
-                                     traded, c_recv.at[z, j], device(r)),
+        start_sized(lambda w: remote(piece(r, w), buf.at[mine, pl.ds(0, w)],
+                                     traded_wide if w == wide else traded, c_recv.at[z, j], device(r)),
                     1 - core if r % 2 else core)
 
     def landed(layer, j, cond=None):
@@ -410,7 +416,7 @@
 
     def carry(layer, j, way, s, cond=None):
         rows = source(layer, j)
-        src = (lambda w: own.at[:, columns(0, w)]) if s == 0 and j == 0 else (lambda w: buf.at[rows, pl.ds(0, w)])
+        src = (lambda w: piece(0, w)) if s == 0 and j == 0 else (lambda w: buf.at[rows, pl.ds(0, w)])
         start_sized(lambda w: remote(src(w), buf.at[rows, pl.ds(0, w)], inward if way else outward,
                                      c_recv.at[layer, j], device(0, -out if way else out)), core, cond)
 
@@ -485,24 +491,21 @@
     send_ids(0, 1, 1)
     send_docs(0, 1, 1, 0, 1, 2)
 
-    part_cols = jnp.where(core == 1, big, small) * 128
-    first = (x * per + core * small) * 128
-    base = doc * width + first
-    reach = jnp.minimum(part_cols, width - first)
-    down = lax.broadcasted_iota(jnp.int32, (GROUP, 128), 0)
+    first = x * turn_at + core * small
+    reach = small + jnp.where(core == 0, 0, jnp.where(x == 0, extra, rest))
+    tail = (core == 1) & (x == 1)
+    lines = lax.broadcasted_iota(jnp.int32, (GROUP, rows_dev), 0)
 
     def prepare_ids(slot):
-        rel = ids[slot] - base
-        rel = jnp.where((rel >= 0) & (rel < reach), rel, -(2**20))
-        tall = jnp.broadcast_to(rel, (GROUP, rows_dev))
-        idb[:, pl.ds(slot * rows_dev, rows_dev)] = tall - lax.broadcasted_iota(jnp.int32, (GROUP, rows_dev), 0)
-
-    buf[mine, pl.ds(0, small * 128)] = own[:, columns(0, small * 128)]
-    if small < big:
-        @pl.when(core == 1)
-        def _():
-            start_col = pl.multiple_of((x * per + 2 * small) * 128, 128)
-            buf[mine, pl.ds(small * 128, 128)] = own[:, pl.ds(start_col, 128)]
+        local = ids[slot] - doc * width
+        rel = jnp.where((local >= first) & (local < first + reach), local - first, -(2**20))
+        rel = jnp.where((local >= half) & (local < turn_at) & tail, local - half + small + rest, rel)
+        idb[:, pl.ds(slot * rows_dev, rows_dev)] = jnp.broadcast_to(rel, (GROUP, rows_dev)) - lines
+
+    def place(w):
+        buf[mine, pl.ds(0, w)] = ends[x] if w == wide else piece(0, w)[...]
+
+    sized(core, None, place)
 
     k1_at = pl.multiple_of(jnp.where(upper, depth - k1, 0), 256)
     k2_at = pl.multiple_of(jnp.where(upper, late, k1), 256)
@@ -622,8 +625,6 @@
             for n, at in enumerate(spots):
                 v = (acc[rows, at] + prod[c:c + GROUP, n * 128:n * 128 + 128]) * by
                 hits[n] = jnp.where(idb[:, at] == c0 + c, v, hits[n])
-                if c0 + c + 128 > small * 128:
-                    v = jnp.where(down < reach - (c0 + c), v, -3.0e38)
                 tops[n] = jnp.maximum(tops[n], v)
         for n, at in enumerate(spots):
             mx[:, at], ch[:, at] = tops[n], hits[n]
@@ -684,15 +685,16 @@
     sized(core, inner, lambda w: sent(buf.at[pl.ds(0, 3 * layer), pl.ds(0, w)], outward))
     sized(core, inner, lambda w: sent(buf.at[pl.ds(0, 2 * layer), pl.ds(0, w)], inward))
     sized(core, end, lambda w: sent(buf.at[pl.ds(0, layer), pl.ds(0, w)], inward))
-    sized(core, None, lambda w: sent(own.at[:, pl.ds(0, 2 * per * 128 - w)], traded))
+    for w, sem, two in ((wide, traded_wide, 0), (small, traded, 1)):
+        pl.when(core == two)(lambda: sent(buf.at[pl.ds(0, 2 * feat), pl.ds(0, w)], sem))
+        pl.when(core != two)(lambda: sent(buf.at[pl.ds(0, feat), pl.ds(0, w)], sem))
 
 
 def by_layers(docs, centroids, assigned):
     nz = lax.axis_size("clu") // 4
     rows_dev, depth = docs.shape
     width, feat = centroids.shape
-    tiles = -(-width // 128)
-    wide = (tiles // 2 - tiles // 4) * 128
+    wide = width // 512 * 128 + width // 2 % 128
     any_space = pl.BlockSpec(memory_space=pl.ANY)
     vmem = pl.BlockSpec(memory_space=pltpu.VMEM)
     dma = pltpu.SemaphoreType.DMA
@@ -703,8 +705,9 @@
         in_specs=[any_space] * 3,
         out_specs=(vmem, vmem),
         scratch_shapes=[
-            pltpu.VMEM((feat, tiles * 128), jnp.bfloat16),
-            pltpu.VMEM((feat, width % 128 or 128), jnp.bfloat16),
+            pltpu.VMEM((feat, width // 128 * 128), jnp.bfloat16),
+            pltpu.VMEM((feat, width % 128), jnp.bfloat16),
+            pltpu.VMEM((2, feat, wide), jnp.bfloat16),
             pltpu.VMEM((depth, wide), jnp.bfloat16),
             pltpu.VMEM((8, rows_dev, depth), jnp.bfloat16),
             pltpu.VMEM((depth, 8 * rows_dev), jnp.bfloat16),
@@ -718,7 +721,7 @@
             pltpu.VMEM((wide, 128), jnp.float32),
             pltpu.VMEM((8, 2, rows_dev), jnp.float32),
             pltpu.VMEM((8, 2, rows_dev), jnp.float32),
-            dma((4,)), dma((6,)), dma((nz, 4)), dma((3,)), dma((12,)), dma((4,)), dma,
+            dma((6,)), dma((7,)), dma((nz, 4)), dma((3,)), dma((12,)), dma((4,)), dma,
         ],
         compiler_params=pltpu.CompilerParams(collective_id=0, has_side_effects=True),
         name="layer_distances",
@@ -727,11 +730,12 @@
 
 
 def fits_layers(docs, centroids):
-    tiles = -(-centroids.shape[0] // 128)
     n_clu, feat = lax.axis_size("clu"), centroids.shape[1]
-    return (lax.axis_size("doc") == 2 and n_clu == 16 and tiles % 2 == 0 and tiles >= 20
-            and feat % 16 == 0 and docs.shape[0] % 128 == 0 and docs.shape[1] % 256 == 0
-            and docs.shape[1] == n_clu * feat == 3 * 256)
+    width = centroids.shape[0]
+    count, extra = width // 2 // 128, width // 2 % 128
+    return (lax.axis_size("doc") == 2 and n_clu == 16 and feat % 16 == 0
+            and width % 2 == 0 and count % 2 == 0 and count >= 10 and extra > 64 and extra % GROUP == 0
+            and docs.shape[0] % 128 == 0 and docs.shape[1] == n_clu * feat == 3 * 256)
 
 
 def on_device(docs, centroids, assigned):

time: 28.9 us -> 28.9 us (level)
  no operation moved by 1% of the time
where the time goes in v8:
time: 28.9 us; the launch traced here: 28.7 us
  Pallas kernels  27.5 us (95%)
  between operations  0.64 us (2%)
  other arithmetic  0.57 us (2%)
    pallas_call x1, Pallas kernels, by_layers(): pl.pallas_call(functools.partial(layer_kernel, nz, feat), out_shape=(line...  27.5 us

profile of v8, /device:TPU:0, one launch (start us, length us, event | category | flops | bytes accessed | tf_op | source)
XLA Modules:
  0.0 28.7 jit_solution(3927827156322264910)
XLA Ops:
  0.6 27.5 %layer_distances.1 = (f32[1,256]{1,0:T(1,128)S(1)}, f32[1,256]{1,0:T(1,128)S(1)}) custom-call(bf16[256,768]{1,0:T(8,128)(2,1)} %docs_in.1, bf16[48,2752]{1,0:T(8,128)(2,1)} %bitcast.4, s32[1,256]{1,0:T(1,128)} %bitcast.5), custom_call_target="tpu_custom_call" | custom-call | tf_op jit(solution)/shard_map/layer_distances/pallas_call | solution.py:702
  28.2 0.6 %broadcast_subtract_fusion = (f32[1,256]{1,0:T(1,128)}, f32[1,256]{1,0:T(1,128)}) fusion(f32[1,256]{1,0:T(1,128)S(1)} %get-tuple-element.5, f32[1,256]{1,0:T(1,128)S(1)} %get-tuple-element.4), kind=kLoop, calls=%fused_computation | loop fusion | flops 512 | bytes 4096 | tf_op jit(solution)/shard_map/sub | solution.py:729

commit v9 on v8

--- a/solution.py
+++ b/solution.py
@@ -537,13 +537,17 @@
         where_docs = pl.ds(slot * rows_dev, count * rows_dev)
 
         def add(w):
-            prod = times(phases[0], 0, w, slot, count)
-            for i in phases[1:]:
-                prod = prod + times(i, 0, w, slot, count)
-            if phases[0]:
-                acc[pl.ds(0, w), where_docs] += prod
-            else:
-                acc[pl.ds(0, w), where_docs] = prod
+            cut_at = w if count > 1 else w // 32 * 16
+            for c, h in ((0, cut_at), (cut_at, w - cut_at)):
+                if not h:
+                    continue
+                prod = times(phases[0], c, h, slot, count)
+                for i in phases[1:]:
+                    prod = prod + times(i, c, h, slot, count)
+                if phases[0]:
+                    acc[pl.ds(c, h), where_docs] += prod
+                else:
+                    acc[pl.ds(c, h), where_docs] = prod
 
         sized(core, None, add)
 
@@ -556,6 +560,7 @@
     relay(1)
     have_docs(2, 0)
     send_docs(2, 6, 4, 0)
+    share(2, 0)
     have_ids(4)
     send_ids(4, 6, 2)
     send_ids(4, 5, 1)
@@ -564,14 +569,16 @@
     relay(2)
     have_docs(4, 1)
     send_docs(4, 6, 2, 1)
+    share(4, 1)
     have_docs(1, 0, 1, 2)
     flatten(1)
     relay(3)
     relay_far(0)
     have_docs(2, 1, 2)
-    share(2, 0, 1, 2)
+    share(2, 1, 2)
     have_docs(4, 2)
     send_docs(4, 6, 2, 2)
+    share(4, 2)
     have_ids(6)
     send_ids(6, 7, 1)
     relay_far(1)
@@ -582,30 +589,31 @@
     for slot in (1, 2, 3, 4, 5, 6, 7):
         prepare_ids(slot)
     relay_far(2)
-    have_docs(4, 0)
-    share(4, 0, 1, 2)
-    relay_far(3)
-    send_last(core == 0)
     have_docs(3, 0, 1, 2)
     flatten(3)
     begin(2, 2, 0)
+    have_docs(4, 0)
+    share(4, 0)
+    flatten(4)
+    relay_far(3)
+    send_last(core == 0)
     gather(1)
-    send_last(core == 1)
-    flatten(4)
     begin(0, 2, 1)
     begin(2, 2, 1)
 
     def share_far():
         for p in (1, 2, 0):
             have_docs(6, p)
-        share(6, 0, 1, 2)
+            share(6, p)
 
     pl.when(core == 1)(share_far)
     have_docs(5, 0, 1, 2)
     flatten(5)
+    begin(4, 2, 0, 1)
+    send_last(core == 1)
     pl.when(core == 0)(share_far)
-    begin(4, 2, 0, 1)
     flatten(6)
+    begin(6, 1, 0, 1)
 
     def scales(c, w):
         total = jnp.sum(csq[:, pl.ds(c, w)] + squares(2, c, w), 0, keepdims=True)
@@ -650,7 +658,7 @@
     landed(z - 3 * out, 1, end)
     have_docs(7, 0, 1, 2)
     flatten(7)
-    begin(6, 2, 0, 1)
+    begin(7, 1, 0, 1)
 
     def advance(k, have):
         c, w = cuts[have][k], cuts[have][k + 1] - cuts[have][k]

time: 28.9 us -> 28.5 us (0.986)
  Pallas kernels: 27.5 us -> 27.1 us
    pallas_call x1, Pallas kernels: 27.5 us -> 27.1 us  [by_layers(): pl.pallas_call(functools.partial(layer_kernel, nz, feat), out_shape=(line...]
where the time goes in v9:
time: 28.5 us; the launch traced here: 28.3 us
  Pallas kernels  27.1 us (95%)
  between operations  0.64 us (2%)
  other arithmetic  0.57 us (2%)
    pallas_call x1, Pallas kernels, by_layers(): pl.pallas_call(functools.partial(layer_kernel, nz, feat), out_shape=(line...  27.1 us

profile of v9, /device:TPU:0, one launch (start us, length us, event | category | flops | bytes accessed | tf_op | source)
XLA Modules:
  0.0 28.3 jit_solution(11328192819539066273)
XLA Ops:
  0.6 27.1 %layer_distances.1 = (f32[1,256]{1,0:T(1,128)S(1)}, f32[1,256]{1,0:T(1,128)S(1)}) custom-call(bf16[256,768]{1,0:T(8,128)(2,1)} %docs_in.1, bf16[48,2752]{1,0:T(8,128)(2,1)} %bitcast.4, s32[1,256]{1,0:T(1,128)} %bitcast.5), custom_call_target="tpu_custom_call" | custom-call | tf_op jit(solution)/shard_map/layer_distances/pallas_call | solution.py:710
  27.7 0.6 %broadcast_subtract_fusion = (f32[1,256]{1,0:T(1,128)}, f32[1,256]{1,0:T(1,128)}) fusion(f32[1,256]{1,0:T(1,128)S(1)} %get-tuple-element.5, f32[1,256]{1,0:T(1,128)S(1)} %get-tuple-element.4), kind=kLoop, calls=%fused_computation | loop fusion | flops 512 | bytes 4096 | tf_op jit(solution)/shard_map/sub | solution.py:737

commit v10 on v9

--- a/solution.py
+++ b/solution.py
@@ -485,9 +485,6 @@
     send_ids(0, 2, 2)
     send_docs(0, 2, 2, 0)
     send_docs(0, 2, 2, 1, 2)
-    send_ids(0, 4, 4)
-    for p in (1, 2, 0):
-        send_docs(0, 4, 4, p)
     send_ids(0, 1, 1)
     send_docs(0, 1, 1, 0, 1, 2)
 
@@ -551,10 +548,17 @@
 
         sized(core, None, add)
 
+    def cross_docs():
+        send_ids(0, 4, 4)
+        for p in (1, 2, 0):
+            send_docs(0, 4, 4, p)
+
     spread(1)
+    pl.when(core == 0)(cross_docs)
     prepare_ids(0)
     flatten(0)
     spread(2)
+    pl.when(core == 1)(cross_docs)
     relay(0)
     spread(3)
     relay(1)
@@ -574,11 +578,11 @@
     flatten(1)
     relay(3)
     relay_far(0)
-    have_docs(2, 1, 2)
-    share(2, 1, 2)
     have_docs(4, 2)
     send_docs(4, 6, 2, 2)
     share(4, 2)
+    have_docs(2, 1, 2)
+    share(2, 1, 2)
     have_ids(6)
     send_ids(6, 7, 1)
     relay_far(1)
@@ -606,12 +610,12 @@
             have_docs(6, p)
             share(6, p)
 
-    pl.when(core == 1)(share_far)
     have_docs(5, 0, 1, 2)
     flatten(5)
+    pl.when(core == 0)(share_far)
     begin(4, 2, 0, 1)
     send_last(core == 1)
-    pl.when(core == 0)(share_far)
+    pl.when(core == 1)(share_far)
     flatten(6)
     begin(6, 1, 0, 1)
 

time: 28.5 us -> 28.4 us (level)
  no operation moved by 1% of the time
where the time goes in v10:
time: 28.4 us; the launch traced here: 28.3 us
  Pallas kernels  27.1 us (95%)
  between operations  0.64 us (2%)
  other arithmetic  0.57 us (2%)
    pallas_call x1, Pallas kernels, by_layers(): pl.pallas_call(functools.partial(layer_kernel, nz, feat), out_shape=(line...  27.1 us
    sub x1, other arithmetic, by_layers(): return (1.0 - near.reshape(rows_dev), 1.0 - chosen.reshape(rows_dev))  0.57 us

profile of v10, /device:TPU:0, one launch (start us, length us, event | category | flops | bytes accessed | tf_op | source)
XLA Modules:
  0.0 28.3 jit_solution(13944464132612791008)
XLA Ops:
  0.6 27.1 %layer_distances.1 = (f32[1,256]{1,0:T(1,128)S(1)}, f32[1,256]{1,0:T(1,128)S(1)}) custom-call(bf16[256,768]{1,0:T(8,128)(2,1)} %docs_in.1, bf16[48,2752]{1,0:T(8,128)(2,1)} %bitcast.4, s32[1,256]{1,0:T(1,128)} %bitcast.5), custom_call_target="tpu_custom_call" | custom-call | tf_op jit(solution)/shard_map/layer_distances/pallas_call | solution.py:714
  27.7 0.6 %broadcast_subtract_fusion = (f32[1,256]{1,0:T(1,128)}, f32[1,256]{1,0:T(1,128)}) fusion(f32[1,256]{1,0:T(1,128)S(1)} %get-tuple-element.5, f32[1,256]{1,0:T(1,128)S(1)} %get-tuple-element.4), kind=kLoop, calls=%fused_computation | loop fusion | flops 512 | bytes 4096 | tf_op jit(solution)/shard_map/sub | solution.py:741

commit v11 on v10

--- a/solution.py
+++ b/solution.py
@@ -306,7 +306,7 @@
     late = -(-4 * feat // 256) * 256
     k1 = 8 * feat // 256 * 256
     k2 = depth - late - k1
-    a = rows_dev * 5 // 16 // 16 * 16
+    a = rows_dev * 3 // 8 // 16 * 16
     b = (rows_dev - a) // 32 * 16
     spans = ((0, a), (a, b), (a + b, rows_dev - a - b))
     cuts = {w: (0, 256, (w - 1) // 256 * 256, w) for w in (small, wide)}

time: 28.4 us -> 28.4 us (level)
  no operation moved by 1% of the time
where the time goes in v11:
time: 28.4 us; the launch traced here: 28.2 us
  Pallas kernels  27 us (95%)
  between operations  0.64 us (2%)
  other arithmetic  0.57 us (2%)
    pallas_call x1, Pallas kernels, by_layers(): pl.pallas_call(functools.partial(layer_kernel, nz, feat), out_shape=(line...  27 us
    sub x1, other arithmetic, by_layers(): return (1.0 - near.reshape(rows_dev), 1.0 - chosen.reshape(rows_dev))  0.57 us

profile of v11, /device:TPU:0, one launch (start us, length us, event | category | flops | bytes accessed | tf_op | source)
XLA Modules:
  0.0 28.2 jit_solution(5437843923992959184)
XLA Ops:
  0.6 27.0 %layer_distances.1 = (f32[1,256]{1,0:T(1,128)S(1)}, f32[1,256]{1,0:T(1,128)S(1)}) custom-call(bf16[256,768]{1,0:T(8,128)(2,1)} %docs_in.1, bf16[48,2752]{1,0:T(8,128)(2,1)} %bitcast.4, s32[1,256]{1,0:T(1,128)} %bitcast.5), custom_call_target="tpu_custom_call" | custom-call | tf_op jit(solution)/shard_map/layer_distances/pallas_call | solution.py:714
  27.7 0.6 %broadcast_subtract_fusion = (f32[1,256]{1,0:T(1,128)}, f32[1,256]{1,0:T(1,128)}) fusion(f32[1,256]{1,0:T(1,128)S(1)} %get-tuple-element.5, f32[1,256]{1,0:T(1,128)S(1)} %get-tuple-element.4), kind=kLoop, calls=%fused_computation | loop fusion | flops 512 | bytes 4096 | tf_op jit(solution)/shard_map/sub | solution.py:741
